TPU v7x, 128 devices: a whole 4x4x4 slice. The times are simulated.
128 devices in a mesh: pb: 4 (over y), db: 32 (over z, x, core).
Axes of the slice: x: 4, y: 4, z: 4, core: 2. Of those that a mesh axis runs over, the one named last changes fastest.
Arguments:
- slab: float32 [262144, 1024], P('db', 'pb'), may hold values from -6 to 6
- queries: float32 [512, 1024], P('db', 'pb'), may hold values from -6 to 6
- block_ids: int32 [512, 16], P('db'), may hold values from 0 to 16383, as said below
Outputs:
- scores: float32 [512, 256], P('db')
- gram: float32 [512, 256, 256], P('db', 'pb')
- penalty: float32 [512, 256, 256], P('db', 'pb')
Inputs may be any that keep to these rules, and one draw needn't show every extreme that they name: `block_ids`: block id k lies in the slab rows of db index k // 512. Among the ids of the 16 queries of one db index, no db index is named more than 12 times, and one db index, the same for all db indices, is named exactly 12 times.
All inputs are finite; a program needn't handle non-finite values.
Results may differ from a plain program's by a relative error of at most 0.000096.
Values sent between devices are 32-bit elements; how exact they have to be, the bound alone decides.
A program may use at most 128 MiB of HBM per device.

v0:
```python
import math

import jax
import jax.numpy as jnp
from jax import lax
from jax.sharding import PartitionSpec as P

BLOCK = 16


epsilon = 1e-06


def from_everyone(x, axis):
    count = lax.axis_size(axis)
    return lax.all_to_all(jnp.broadcast_to(x[None], (count, *x.shape)), axis, 0, 0, tiled=True)


def over_copies(x, axis):
    everything = from_everyone(x, axis)
    return jnp.sum(everything, axis=0)


def together(arrays, axis):
    vector, at, done = (jnp.concatenate([a.reshape(-1) for a in arrays]), 0, [])
    running = over_copies(vector, axis)
    for a in arrays:
        done.append(running[at : at + a.size].reshape(a.shape))
        at += a.size
    return tuple(done)


def per_device(slab, queries, block_ids):
    highest = lax.Precision.HIGHEST
    query_count, width_part = queries.shape
    db_count = lax.axis_size("db")
    pb_count = lax.axis_size("pb")
    full_width = width_part * pb_count
    blocks_named = block_ids.shape[1]
    cand_count = blocks_named * BLOCK
    own_count = cand_count // pb_count
    blocks_each = slab.shape[0] // BLOCK
    request_count = query_count * blocks_named
    capacity = 3 * request_count // (2 * db_count)
    flat_ids = block_ids.reshape(request_count)
    owners = flat_ids // blocks_each
    local_block = flat_ids % blocks_each
    onehot = (owners[:, None] == jnp.arange(db_count, dtype=jnp.int32)[None, :]).astype(jnp.int32)
    slot_index = jnp.sum((jnp.cumsum(onehot, axis=0) - 1) * onehot, axis=1)
    requests = jnp.zeros((db_count, capacity), jnp.int32).at[owners, slot_index].set(local_block)
    slab_blocks = slab.reshape(blocks_each, BLOCK, width_part)
    found = slab_blocks[lax.all_to_all(requests, "db", split_axis=0, concat_axis=0, tiled=True)]
    replies = lax.all_to_all(found, "db", split_axis=0, concat_axis=0, tiled=True)
    flat_replies = replies.reshape(db_count * capacity, BLOCK, width_part)
    cand_rows = flat_replies[owners * capacity + slot_index].reshape(
        query_count, cand_count, width_part
    )
    own_start = lax.axis_index("pb") * own_count
    query_dots = jnp.einsum("qcw,qw->qc", cand_rows, queries, precision=highest)
    row_squares = jnp.sum(cand_rows * cand_rows, axis=2)
    query_squares = jnp.sum(queries * queries, axis=1)
    query_dots, row_squares, query_squares = together(
        (query_dots, row_squares, query_squares), "pb"
    )
    partial_gram = jnp.einsum("qiw,qjw->qij", cand_rows, cand_rows, precision=highest)
    raw_gram = lax.psum_scatter(partial_gram, "pb", scatter_dimension=1, tiled=True)
    query_norm = jnp.sqrt(query_squares + epsilon)
    row_norm = jnp.sqrt(row_squares + epsilon)
    scores = math.sqrt(full_width) * query_dots / (query_norm[:, None] * row_norm)
    own_norm = lax.dynamic_slice_in_dim(row_norm, own_start, own_count, 1)
    own_scores = lax.dynamic_slice_in_dim(scores, own_start, own_count, 1)
    gram = raw_gram / (own_norm[:, :, None] * row_norm[:, None, :])
    penalty = gram * jax.nn.sigmoid(scores[:, None, :] - own_scores[:, :, None])
    return (scores, gram, penalty)


def solution(mesh):
    return jax.shard_map(
        per_device,
        mesh=mesh,
        in_specs=(P("db", "pb"), P("db", "pb"), P("db", None)),
        out_specs=(P("db", None), P("db", "pb", None), P("db", "pb", None)),
        check_vma=False,
    )
```

profile of v0, /device:TPU:1, one launch (start us, length us, event | category | flops | bytes accessed | tf_op | source)
XLA Modules:
  0.0 200.1 jit_solution(12594656421256675537)
XLA Ops:
  7.2 0.8 reshape.259
  7.9 0.8 reshape.258
  8.7 0.8 reshape.257
  9.5 0.6 reduce-window.6
  10.1 0.2 slice_reduce_fusion
  10.4 0.1 fusion.1
  10.5 12.8 %scatter_fusion = s32[32,12]{0,1:T(8,128)S(1)} fusion(s32[32,12]{0,1:T(8,128)S(1)} %broadcast.241, s32[256]{0:T(256)S(1)} %bitcast.39, s32[256]{0:T(256)S(1)} %get-tuple-element.9), kind=kCustom, calls=%fused_computation.2 | custom fusion | bytes 5120 | tf_op jit(solution)/shard_map/scatter | solution.py:50
  23.3 0.1 copy.13
  23.4 16.2 %all_to_all.23 = s32[32,1,12]{2,1,0:T(1,128)S(1)} all-to-all(s32[32,1,12]{2,1,0:T(1,128)S(1)} %copy.13), channel_id=1, replica_groups=mesh['pb'=4,'db'=32] {'db'}, dimensions={0} | all-to-all | bytes 3072 | tf_op jit(solution)/shard_map/all_to_all | solution.py:52
  39.5 0.1 reshape.267
  39.7 7.0 %gather_fusion = f32[384,16,256]{2,1,0:T(8,128)} fusion(f32[512,16,256]{2,1,0:T(8,128)} %bitcast.40, s32[1024]{0:T(1024)S(1)} %pad_clamp_fusion.1), kind=kCustom, calls=%fused_computation | custom fusion | bytes 12584448 | tf_op jit(solution)/shard_map/gather | solution.py:52
  46.7 5.1 %all-to-all-start.1 = ((f32[32,12,16,256]{3,2,1,0:T(8,128)}), f32[32,12,16,256]{3,2,1,0:T(8,128)}, u32[]{:S(2)}, u32[]{:S(2)}) async-start(f32[32,12,16,256]{3,2,1,0:T(8,128)} %bitcast.38), calls=%async_computation.1 | async-start | bytes 12582912 | tf_op jit(solution)/shard_map/all_to_all | solution.py:53
  51.8 0.0 reduce-scatter.2.cloned.1.call-start
  51.9 73.3 %all-to-all-done.1 = f32[32,12,16,256]{3,2,1,0:T(8,128)} async-done(((f32[32,12,16,256]{3,2,1,0:T(8,128)}), f32[32,12,16,256]{3,2,1,0:T(8,128)}, u32[]{:S(2)}, u32[]{:S(2)}) %all-to-all-start.1) | async-done | bytes 6291488 | tf_op jit(solution)/shard_map/all_to_all | solution.py:53
  125.1 5.6 %gather_fusion.1 = f32[256,16,256]{2,1,0:T(8,128)} fusion(f32[384,16,256]{2,1,0:T(8,128)} %bitcast.7, s32[1024]{0:T(1024)S(1)} %pad_clamp_fusion), kind=kCustom, calls=%fused_computation.1 | custom fusion | bytes 8389632 | tf_op jit(solution)/shard_map/gather | solution.py:55
  130.8 9.6 %fusion.8 = f32[16,256,256]{2,1,0:T(8,128)} fusion(f32[16,256,256]{2,1,0:T(8,128)} %bitcast.36), kind=kOutput, calls=%fused_computation.52 | convolution fusion | flops 3221225472 | bytes 8388608 | tf_op jit(solution)/shard_map/qiw,qjw->qij/dot_general | solution.py:65
  140.4 0.0 reduce-scatter.2.cloned.1.call-update
  140.4 0.7 copy-done.2
  141.1 0.1 multiply_reduce_fusion.1
  141.2 5.9 %fusion.4 = f32[16,1,256]{2,1,0:T(1,128)S(1)} fusion(f32[16,256,256]{2,1,0:T(8,128)} %bitcast.37, f32[16,256,1]{1,0,2:T(8,128)S(1)} %bitcast.41), kind=kOutput, calls=%fused_computation.20 | convolution fusion | flops 12582912 | bytes 4227072 | tf_op jit(solution)/shard_map/qcw,qw->qc/dot_general | solution.py:59
  147.2 0.0 copy-done
  147.2 0.6 multiply_reduce_fusion
  147.8 0.1 reshape.264
  147.9 0.7 broadcast_in_dim.2
  148.7 4.2 %all-to-all-start.2 = ((f32[4,1,8208]{2,1,0:T(1,128)}), f32[4,1,8208]{2,1,0:T(1,128)S(1)}, u32[]{:S(2)}, u32[]{:S(2)}) async-start(f32[4,1,8208]{2,1,0:T(1,128)} %broadcast_in_dim.2), calls=%async_computation.2 | async-start | bytes 266240 | tf_op jit(solution)/shard_map/all_to_all | solution.py:16
  152.8 6.4 %all-to-all-done.2 = f32[4,1,8208]{2,1,0:T(1,128)S(1)} async-done(((f32[4,1,8208]{2,1,0:T(1,128)}), f32[4,1,8208]{2,1,0:T(1,128)S(1)}, u32[]{:S(2)}, u32[]{:S(2)}) %all-to-all-start.2) | async-done | bytes 131360 | tf_op jit(solution)/shard_map/all_to_all | solution.py:16
  159.3 0.1 reduce_sum.42
  159.5 0.1 multiply_divide_fusion.1
  159.6 0.1 constant_dynamic-slice_fusion
  159.6 30.6 %reduce-scatter.2.cloned.1.call-done = f32[16,64,256]{2,1,0:T(8,128)} async-done(((f32[16,256,256]{2,1,0:T(8,128)}), f32[16,64,256]{2,1,0:T(8,128)}) %reduce-scatter.2.cloned.1.call-update) | async-done | bytes 1048592 | tf_op jit(solution)/shard_map/reduce_scatter | solution.py:66
  190.2 3.0 %divide_multiply_fusion = (f32[16,64,256]{2,1,0:T(8,128)}, f32[16,64,256]{2,1,0:T(8,128)}) fusion(f32[16,64]{1,0:T(8,128)S(1)} %get-tuple-element.11, f32[16,256]{1,0:T(8,128)S(1)} %multiply_divide_fusion.1, f32[16,64,256]{2,1,0:T(8,128)} %reduce-scatter.2.cloned.1.call-done, f32[16,256]{1,0:T(8,128)S(1)} %sqrt.18, f32[16,64]{1,0:T(8,128)S(1)} %get-tuple-element.12), kind=kLoop, calls=%fused_computation.4 | loop fusion | flops 1835008 | bytes 3186688 | tf_op jit(solution)/shard_map/mul | solution.py:73
  193.2 0.0 copy-done.1
  (21 shorter events, 0.2 us)
Async XLA Ops:
  46.7 78.5 %all-to-all-start.1 = ((f32[32,12,16,256]{3,2,1,0:T(8,128)}), f32[32,12,16,256]{3,2,1,0:T(8,128)}, u32[]{:S(2)}, u32[]{:S(2)}) async-start(f32[32,12,16,256]{3,2,1,0:T(8,128)} %bitcast.38), calls=%async_computation.1 | async-start | bytes 12582912 | tf_op jit(solution)/shard_map/all_to_all | solution.py:53
  51.8 138.4 %reduce-scatter.2.cloned.1.call-start = ((), (), s32[]{:S(2)}) async-start(), calls=%async_computation.4 | async-start | bytes 5242880 | tf_op jit(solution)/shard_map/reduce_scatter | solution.py:66
  140.4 0.7 copy-start.2
  141.1 6.1 %copy-start = (f32[256,16,256]{2,1,0:T(8,128)S(1)}, f32[256,16,256]{2,1,0:T(8,128)}, u32[]{:S(2)}) copy-start(f32[256,16,256]{2,1,0:T(8,128)} %gather_fusion.1) | copy-start | bytes 12582916
  148.7 10.6 %all-to-all-start.2 = ((f32[4,1,8208]{2,1,0:T(1,128)}), f32[4,1,8208]{2,1,0:T(1,128)S(1)}, u32[]{:S(2)}, u32[]{:S(2)}) async-start(f32[4,1,8208]{2,1,0:T(1,128)} %broadcast_in_dim.2), calls=%async_computation.2 | async-start | bytes 266240 | tf_op jit(solution)/shard_map/all_to_all | solution.py:16
  159.6 33.7 %copy-start.1 = (f32[16,256]{1,0:T(8,128)}, f32[16,256]{1,0:T(8,128)S(1)}, u32[]{:S(2)}) copy-start(f32[16,256]{1,0:T(8,128)S(1)} %multiply_divide_fusion.1) | copy-start | bytes 49156
Sparse Core Ops, SparseCore 0:
  140.5 49.6 reduce-scatter.1
where the time goes:
time: 201 us; the launch traced here: 200 us
  waiting for transfers between devices  110 us (55%)
  local copies, waits for them, and re-layouts  29.8 us (15%)
  blocking collectives  16.2 us (8%)
  matrix products  15.5 us (8%)
  between operations  14.2 us (7%)
  starting transfers between devices  9.35 us (5%)
  other arithmetic  4.78 us (2%)
    all_to_all x1, waiting for transfers between devices, per_device(): lax.all_to_all(found, 'db', split_axis=0, concat_axis=0, tiled=True)  73.3 us
    reduce_scatter x1, waiting for transfers between devices, per_device(): lax.psum_scatter(partial_gram, 'pb', scatter_dimension=1, tiled=True)  30.6 us
    all_to_all x1, blocking collectives, per_device(): lax.all_to_all(requests, 'db', split_axis=0, concat_axis=0, tiled=True)  16.2 us
    scatter x1, local copies, waits for them, and re-layouts, per_device(): jnp.zeros((db_count, capacity), jnp.int32).at[owners, slot_index]  12.8 us
    dot_general x1, matrix products, per_device(): jnp.einsum('qiw,qjw->qij', cand_rows, cand_rows, precision=highest)  9.63 us
    gather x1, local copies, waits for them, and re-layouts, per_device(): slab_blocks[lax.all_to_all(requests, 'db', split_axis=0, concat_axis=0, t...  7 us
    all_to_all x1, waiting for transfers between devices, from_everyone(): lax.all_to_all(jnp.broadcast_to(x[None], (count, *x.shape)), axis, 0, 0,...  6.44 us
    dot_general x1, matrix products, per_device(): query_dots = jnp.einsum('qcw,qw->qc', cand_rows, queries, precision=highest)  5.92 us
  transfers between devices with their start and end apart: 3, of which 3 were waited for; matrix products, arithmetic and copies ran while one was open for 4% of the time, Pallas kernels for 0%

commit v1 on v0

v1 whole, which is shorter than its diff:
```python
import functools
import math

import jax
import jax.numpy as jnp
from jax import lax
from jax.experimental import pallas as pl
from jax.experimental.pallas import tpu as pltpu
from jax.sharding import PartitionSpec as P

BLOCK = 16
CAP = 12
HALF = 6
NZ, NX, NC, NY = 4, 4, 2, 4
EPS = 1e-06
MESH = pl.DeviceIdType.MESH
F32 = jnp.float32
CHUNKS = ((0, 0), (1, 0), (0, 1), (1, 1))
NCH = len(CHUNKS)
WIDE = [(d, e) for d in range(4) for e in range(2) if (d, e) != (0, 0)]


def main_kernel(scale, tab, pos, query, slab, gram_out, score_out, slabv, tmid, tfin, tsm, src_a, mid_a, src_b, mid_b,
                fin0, fin1, fin2, fin3, ysend, cand, qall, acc, sq, dt, grecv, srecv, gsend, ssend,
                lsem, tsem, ts1, tr1, ts2, tr2, s1s, s1r, s2s, s2r, ys, yr, qs, qr, gs, gr, ss, sr):
    fin = (fin0, fin1, fin2, fin3)
    y = lax.axis_index("pb")
    db = lax.axis_index("db")
    z, x, c = db // (NX * NC), (db // NC) % NX, db % NC
    jx = x * NC + c
    jz = z * NC + c

    def dev(yy, zz, xx, cc):
        return (yy, (zz * NX + xx) * NC + cc)

    def up(v, d, n):
        return (v + d) % n

    load = pltpu.make_async_copy(slab, slabv, lsem)
    load.start()

    peers = [dev(y, up(z, d, NZ), x, up(c, e, NC)) for d, e in WIDE]
    peers += [dev(y, z, up(x, d, NX), up(c, e, NC)) for d, e in WIDE if d]
    peers += [dev(up(y, d, NY), z, x, c) for d in range(1, NY)]
    barrier = pltpu.get_barrier_semaphore()
    for p in peers:
        pl.semaphore_signal(barrier, inc=1, device_id=p, device_id_type=MESH)
    pl.semaphore_wait(barrier, len(peers))

    sends = []

    def remote(src, dst, ssem, rsem, target):
        cp = pltpu.make_async_remote_copy(src_ref=src, dst_ref=dst, send_sem=ssem, recv_sem=rsem,
                                          device_id=target, device_id_type=MESH)
        cp.start()
        sends.append(cp)
        return cp

    first = [remote(tab.at[up(z, d, NZ)], tmid.at[z], ts1.at[d - 1], tr1.at[d - 1], dev(y, up(z, d, NZ), x, c))
             for d in range(1, NZ)]
    qcopies = [remote(query.at[up(y, d, NY)], qall.at[y], qs.at[d - 1], qr.at[d - 1], dev(up(y, d, NY), z, x, c))
               for d in range(1, NY)]
    qall[y] = query[y]
    tmid[z] = tab[z]
    for cp in first:
        cp.wait_recv()
    second = []
    for k, (d, e) in enumerate(WIDE):
        x2, c2 = up(x, d, NX), up(c, e, NC)
        second.append(remote(tmid.at[:, x2 * NC + c2], tfin.at[jx], ts2.at[k], tr2.at[k], dev(y, z, x2, c2)))
    tfin[jx] = tmid[:, jx]
    for cp in second:
        cp.wait_recv()
    tcopy = pltpu.make_async_copy(tfin, tsm, tsem)
    tcopy.start()
    tcopy.wait()
    load.wait()

    def gather(ch):
        h, f = CHUNKS[ch]
        rows, lanes = slice(8 * h, 8 * h + 8), slice(128 * f, 128 * f + 128)

        for d in range(4):
            z2, x2 = up(z, d, NZ), up(x, d, NX)

            def body(j, carry):
                to_a = mid_a if d == 0 else src_a
                to_b = mid_b if d == 0 else src_b
                for s in range(HALF):
                    to_a[ch, z2, j, s] = slabv[tsm[j, z2, 0, s], rows, lanes]
                for s in range(HALF):
                    to_b[ch, x2, j, s] = slabv[tsm[x2 * NC + j % NC, j // NC, 0, HALF + s], rows, lanes]
                return carry

            lax.fori_loop(0, 8, body, 0)

    def stage1(ch):
        cps = []
        for d in range(1, 4):
            z2, x2 = up(z, d, NZ), up(x, d, NX)
            cps.append(remote(src_a.at[ch, z2], mid_a.at[ch, z], s1s.at[ch, 0, d - 1], s1r.at[ch, 0, d - 1], dev(y, z2, x, c)))
            cps.append(remote(src_b.at[ch, x2], mid_b.at[ch, x], s1s.at[ch, 1, d - 1], s1r.at[ch, 1, d - 1], dev(y, z, x2, c)))
        return cps

    def stage2(ch, before):
        for cp in before:
            cp.wait_recv()
        cps = []
        for k, (d, e) in enumerate(WIDE):
            z2, x2, c2 = up(z, d, NZ), up(x, d, NX), up(c, e, NC)
            cps.append(remote(mid_a.at[ch, :, x2 * NC + c2], fin[ch].at[:, c, x, 0:HALF], s2s.at[ch, 0, k], s2r.at[ch, 0, k], dev(y, z, x2, c2)))
            cps.append(remote(mid_b.at[ch, :, z2 * NC + c2], fin[ch].at[z, c, :, HALF:CAP], s2s.at[ch, 1, k], s2r.at[ch, 1, k], dev(y, z2, x, c2)))
        for i in range(4):
            fin[ch][i, c, x, 0:HALF] = mid_a[ch, i, jx]
            fin[ch][z, c, i, HALF:CAP] = mid_b[ch, i, jz]
        return cps

    def across(ch, before):
        h, f = CHUNKS[ch]
        for cp in before:
            cp.wait_recv()
        cps = []
        for d in (1, 3, 2, 0):
            y2 = up(y, d, NY)

            def body(i, carry):
                for u in range(8):
                    t = i * 8 + u
                    r = y2 * 64 + t
                    val = fin[ch][pos[0, r], pos[1, r], pos[2, r], pos[3, r]]
                    if d:
                        ysend[ch, d - 1, t] = val
                    else:
                        cand[y, f, t, h] = val
                return carry

            lax.fori_loop(0, 8, body, 0)
            if d:
                cps.append(remote(ysend.at[ch, d - 1], cand.at[y, f, :, h], ys.at[ch, d - 1], yr.at[ch, d - 1], dev(y2, z, x, c)))
        return cps

    def nt(a, b):
        return lax.dot_general(a, b, (((1,), (1,)), ((), ())), preferred_element_type=F32)

    def partial(q, f):
        s2 = jnp.zeros((256, 128), F32)
        dd = jnp.zeros((256, 128), F32)
        g = jnp.zeros((256, 256), F32)
        for yp in range(0, NY, 2):
            his, los = [], []
            for yy in (yp, yp + 1):
                v = cand[yy, f, pl.ds(q * 16, 16)].reshape(256, 128)
                qv = qall[yy, q, :, 128 * f:128 * f + 128]
                s2 = s2 + v * v
                dd = dd + v * qv
                hi = v.astype(jnp.bfloat16)
                his.append(hi)
                los.append((v - hi.astype(F32)).astype(jnp.bfloat16))
            hi = jnp.concatenate(his, axis=1)
            lo = jnp.concatenate(los, axis=1)
            g = g + (nt(hi, hi) + (nt(hi, lo) + nt(lo, hi)))
        return g, s2, dd

    def first_half(q, carry):
        g, s2, dd = partial(q, 0)
        acc[q] = g
        sq[q] = s2
        dt[q] = dd
        return carry

    gather(0)
    a0 = stage1(0)
    gather(1)
    a1 = stage1(1)
    gather(2)
    b0 = stage2(0, a0)
    a2 = stage1(2)
    gather(3)
    b1 = stage2(1, a1)
    a3 = stage1(3)
    c0 = across(0, b0)
    b2 = stage2(2, a2)
    c1 = across(1, b1)
    b3 = stage2(3, a3)
    c2 = across(2, b2)
    for cp in qcopies:
        cp.wait_recv()
    for cp in c0 + c1:
        cp.wait_recv()
    lax.fori_loop(0, 4, first_half, 0)
    c3 = across(3, b3)
    for cp in c2 + c3:
        cp.wait_recv()

    lane = lax.broadcasted_iota(jnp.int32, (256, 128), 1)
    outs = []
    for q in range(4):
        g, s2, dd = partial(q, 1)
        g = g + acc[q]
        rn = 1.0 / jnp.sqrt(jnp.sum(s2 + sq[q], axis=1, keepdims=True) + EPS)
        dots = jnp.sum(dd + dt[q], axis=1, keepdims=True)
        qsum = jnp.zeros((1, 128), F32)
        for yy in range(NY):
            for f in range(2):
                qv = qall[yy, q, :, 128 * f:128 * f + 128]
                qsum = qsum + qv * qv
        qn = jnp.sqrt(jnp.sum(qsum, axis=1, keepdims=True) + EPS)
        score = (scale * dots) * (rn / qn)
        both = jnp.where(lane == 0, rn, score)
        flat = both.T
        gsend[q] = g * rn * flat[0:1, :]
        ssend[q] = flat[1:2, :]
        for d in (1, 3, 2):
            y2 = up(y, d, NY)
            outs.append(remote(gsend.at[q, pl.ds(y2 * 64, 64)], grecv.at[y * 4 + q], gs.at[q, d - 1], gr.at[q, d - 1], dev(y2, z, x, c)))
            outs.append(remote(ssend.at[q], srecv.at[y * 4 + q], ss.at[q, d - 1], sr.at[q, d - 1], dev(y2, z, x, c)))
        grecv[y * 4 + q] = gsend[q, pl.ds(pl.multiple_of(y * 64, 64), 64)]
        srecv[y * 4 + q] = ssend[q]
    for cp in outs:
        cp.wait_recv()
    gram_out[...] = grecv[...]
    score_out[...] = srecv[...]
    for cp in sends:
        cp.wait_send()


def main_call(scale, tab, pos, query, slab):
    dma = pltpu.SemaphoreType.DMA
    vm = pltpu.VMEM
    vmem = pl.BlockSpec(memory_space=pltpu.VMEM)
    return pl.pallas_call(
        functools.partial(main_kernel, scale),
        out_shape=(jax.ShapeDtypeStruct((16, 64, 256), F32), jax.ShapeDtypeStruct((16, 1, 256), F32)),
        in_specs=[vmem, pl.BlockSpec(memory_space=pltpu.SMEM), vmem, pl.BlockSpec(memory_space=pl.ANY)],
        out_specs=(vmem, vmem),
        scratch_shapes=[
            vm(slab.shape, F32),
            vm((4, 8, 1, 128), jnp.int32), vm((8, 4, 1, 128), jnp.int32), pltpu.SMEM((8, 4, 1, 128), jnp.int32),
            vm((NCH, 4, 8, HALF, 8, 128), F32), vm((NCH, 4, 8, HALF, 8, 128), F32),
            vm((NCH, 4, 8, HALF, 8, 128), F32), vm((NCH, 4, 8, HALF, 8, 128), F32),
            *[vm((NZ, NC, NX, CAP, 8, 128), F32) for _ in range(NCH)],
            vm((NCH, 3, 64, 8, 128), F32), vm((NY, 2, 64, 2, 8, 128), F32), vm((NY, 4, 1, 256), F32),
            vm((4, 256, 256), F32), vm((4, 256, 128), F32), vm((4, 256, 128), F32),
            vm((16, 64, 256), F32), vm((16, 1, 256), F32), vm((4, 256, 256), F32), vm((4, 1, 256), F32),
            dma(()), dma(()), dma((3,)), dma((3,)), dma((7,)), dma((7,)),
            dma((NCH, 2, 3)), dma((NCH, 2, 3)), dma((NCH, 2, 7)), dma((NCH, 2, 7)),
            dma((NCH, 3)), dma((NCH, 3)), dma((3,)), dma((3,)), dma((4, 3)), dma((4, 3)), dma((4, 3)), dma((4, 3)),
        ],
        compiler_params=pltpu.CompilerParams(collective_id=0, has_side_effects=True, vmem_limit_bytes=60 * 2**20),
    )(tab, pos, query, slab)


def per_device(slab, queries, block_ids):
    query_count, width_part = queries.shape
    db_count = lax.axis_size("db")
    pb_count = lax.axis_size("pb")
    full_width = width_part * pb_count
    blocks_named = block_ids.shape[1]
    blocks_each = slab.shape[0] // BLOCK
    request_count = query_count * blocks_named
    ids = block_ids.reshape(request_count)
    owner = ids // blocks_each
    local = ids % blocks_each
    k = jnp.arange(request_count, dtype=jnp.int32)
    earlier = (owner[:, None] == owner[None, :]) & (k[None, :] < k[:, None])
    slot = jnp.sum(earlier.astype(jnp.int32), axis=1)
    place = owner * 16 + slot
    wanted = jnp.arange(db_count * 16, dtype=jnp.int32)
    table = jnp.sum(jnp.where(place[None, :] == wanted[:, None], local[None, :], 0), axis=1)
    table = jnp.pad(table.reshape(db_count, 16), ((0, 0), (0, 112))).reshape(NZ, NX * NC, 1, 128)
    pos = jnp.stack([owner // 8, owner % 2, (owner // 2) % 4, slot])
    gram, scores = main_call(math.sqrt(full_width), table, pos, queries.reshape(pb_count, query_count // pb_count, 1, width_part),
                             slab.reshape(blocks_each, BLOCK, width_part))
    scores = scores.reshape(query_count, -1)
    own = lax.dynamic_slice_in_dim(scores, lax.axis_index("pb") * 64, 64, 1)
    penalty = gram * jax.nn.sigmoid(scores[:, None, :] - own[:, :, None])
    return (scores, gram, penalty)


def solution(mesh):
    return jax.shard_map(
        per_device,
        mesh=mesh,
        in_specs=(P("db", "pb"), P("db", "pb"), P("db", None)),
        out_specs=(P("db", None), P("db", "pb", None), P("db", "pb", None)),
        check_vma=False,
    )
```

time: 201 us -> 134 us (0.67)
  Pallas kernels: 0 us -> 122 us
  waiting for transfers between devices: 110 us -> 0 us
  local copies, waits for them, and re-layouts: 29.8 us -> 7.39 us
  blocking collectives: 16.2 us -> 0 us
  matrix products: 15.5 us -> 0 us
  between operations: 14.2 us -> 0.67 us
  starting transfers between devices: 9.35 us -> 0 us
    pallas_call x0 -> x1, Pallas kernels: none -> 122 us  [main_call(): pl.pallas_call(functools.partial(main_kernel, scale), out_shape=(jax.Shap...]
    all_to_all x2 -> x0, waiting for transfers between devices: 79.7 us -> none  [the longest x1 73.3 us: per_device(): lax.all_to_all(found, 'db', split_axis=0, concat_axis=0, tiled=True)]
    reduce_scatter x1 -> x0, waiting for transfers between devices: 30.6 us -> none  [per_device(): lax.psum_scatter(partial_gram, 'pb', scatter_dimension=1, tiled=True)]
    all_to_all x1 -> x0, blocking collectives: 16.2 us -> none  [per_device(): lax.all_to_all(requests, 'db', split_axis=0, concat_axis=0, tiled=True)]
    dot_general x2 -> x0, matrix products: 15.5 us -> none  [the longest x1 9.63 us: per_device(): jnp.einsum('qiw,qjw->qij', cand_rows, cand_rows, precision=highest)]
    scatter x1 -> x0, local copies, waits for them, and re-layouts: 12.8 us -> none  [per_device(): jnp.zeros((db_count, capacity), jnp.int32).at[owners, slot_index]]
    gather x2 -> x0, local copies, waits for them, and re-layouts: 12.6 us -> none  [the longest x1 7 us: per_device(): slab_blocks[lax.all_to_all(requests, 'db', split_axis=0, concat_axis=0, t...]
    all_to_all x2 -> x0, starting transfers between devices: 9.31 us -> none  [the longest x1 5.13 us: per_device(): lax.all_to_all(found, 'db', split_axis=0, concat_axis=0, tiled=True)]
  transfers between devices with their start and end apart: 3 -> 0, of which waited for: 3 -> 0; matrix products, arithmetic and copies ran while one was open for 4% -> 0% of each run, Pallas kernels for 0% -> 0%
where the time goes in v1:
time: 134 us
  Pallas kernels  122 us (91%)
  local copies, waits for them, and re-layouts  7.39 us (6%)
  other arithmetic  3.56 us (3%)
    pallas_call x1, Pallas kernels, main_call(): pl.pallas_call(functools.partial(main_kernel, scale), out_shape=(jax.Shap...  122 us
    unnamed x4, local copies, waits for them, and re-layouts  3.02 us

profile of v1, /device:TPU:1, one launch (start us, length us, event | category | flops | bytes accessed | tf_op | source)
XLA Modules:
  0.0 133.9 jit_solution(9413617224414150377)
XLA Ops:
  0.6 0.8 reshape.326
  1.4 0.8 reshape.323
  2.2 0.2 convert_reduce_fusion
  2.4 0.2 select_reduce_fusion
  2.6 0.6 pad_add_fusion.pos
  3.2 0.1 reshape.324
  3.3 0.6 pad.4
  3.9 1.3 %reshape.327.query = f32[4,4,1,256]{3,2,1,0:T(1,128)} reshape(f32[16,256]{1,0:T(8,128)} %param.4) | data formatting | bytes 32768 | tf_op jit(solution)/shard_map/reshape | solution.py:272
  5.3 122.3 %shard_map.58 = (f32[16,64,256]{2,1,0:T(8,128)}, f32[16,1,256]{2,1,0:T(1,128)}) custom-call(s32[4,8,1,128]{3,2,1,0:T(1,128)} %bitcast.10, s32[4,256]{1,0:T(4,128)} %pad_add_fusion.pos, f32[4,4,1,256]{3,2,1,0:T(1,128)} %reshape.327.query, f32[512,16,256]{2,1,0:T(8,128)} %bitcast.7), custom_call_target="tpu_custom_call" | custom-call | tf_op jit(solution)/shard_map/pallas_call | solution.py:231
  127.5 0.8 constant_dynamic-slice_fusion
  128.3 0.7 copy.8
  129.0 0.0 copy-start
  129.0 2.6 %divide_multiply_fusion = f32[16,64,256]{2,1,0:T(8,128)} fusion(f32[16,64,256]{2,1,0:T(8,128)} %get-tuple-element.17, f32[16,64]{1,0:T(8,128)S(1)} %bitcast.11, f32[16,256]{1,0:T(8,128)S(1)} %bitcast.8), kind=kLoop, calls=%fused_computation | loop fusion | flops 1310720 | bytes 2117632 | tf_op jit(solution)/shard_map/mul | solution.py:276
  131.6 2.3 %copy.10 = f32[16,64,256]{2,1,0:T(8,128)} copy(f32[16,64,256]{2,1,0:T(8,128)} %get-tuple-element.17) | data formatting | bytes 2097152
  133.9 0.0 copy-done
  (5 shorter events, 0.1 us)
Async XLA Ops:
  129.0 4.8 %copy-start = (f32[16,1,256]{2,0,1:T(8,128)}, f32[16,1,256]{2,0,1:T(8,128)S(1)}, u32[]{:S(2)}) copy-start(f32[16,1,256]{2,0,1:T(8,128)S(1)} %copy.8) | copy-start | bytes 49156

commit v2 on v1

v2 whole, which is shorter than its diff:
```python
import functools
import math

import jax
import jax.numpy as jnp
from jax import lax
from jax.experimental import pallas as pl
from jax.experimental.pallas import tpu as pltpu
from jax.sharding import PartitionSpec as P

BLOCK = 16
CAP = 12
HALF = 6
NZ, NX, NC, NY = 4, 4, 2, 4
EPS = 1e-06
MESH = pl.DeviceIdType.MESH
F32 = jnp.float32
CHUNKS = ((8, 0, 0), (8, 8, 0), (4, 0, 1), (4, 4, 1), (4, 0, 2), (4, 4, 2))
NCH = len(CHUNKS)
STEPS = ((1, 0), (1, 1), (2, 0), (1, 2), (2, 1), (1, 3), (3, 0), (2, 2), (1, 4), (3, 1), (2, 3), (1, 5), (3, 2), ("wait", 0), ("wait", 1),
         ("sum", 0, 0), ("sum", 0, 1), (2, 4), ("sum", 0, 2), ("sum", 0, 3), (3, 3), (2, 5), ("wait", 2), ("wait", 3),
         ("sum", 1, 0), ("sum", 1, 1), ("sum", 1, 2), ("sum", 1, 3), (3, 4), (3, 5))
WIDE = [(d, e) for d in range(4) for e in range(2) if (d, e) != (0, 0)]


def main_kernel(scale, ids, query, slab, part_out, vec_out, slabv, idv, qall, qrow, tab, tmid, tfin, tsm, pos, psm, *rest):
    src_a, mid_a, src_b, mid_b, fin, ysend, cand = (rest[i * NCH:(i + 1) * NCH] for i in range(7))
    (acc, sq, dt, gsend, ssend,
     lsem, isem, psem, tsem, qsem, ts1, tr1, ts2, tr2, s1s, s1r, s2s, s2r, ys, yr, zs, zr, qs, qr, gs, gr, ss, sr) = rest[7 * NCH:]
    y = lax.axis_index("pb")
    db = lax.axis_index("db")
    z, x, c = db // (NX * NC), (db // NC) % NX, db % NC
    jx = x * NC + c
    jz = z * NC + c

    def dev(yy, zz, xx, cc):
        return (yy, (zz * NX + xx) * NC + cc)

    def up(v, d, n):
        return (v + d) % n

    peers = [dev(y, up(z, d, NZ), x, up(c, e, NC)) for d, e in WIDE]
    peers += [dev(y, z, up(x, d, NX), up(c, e, NC)) for d, e in WIDE if d]
    peers += [dev(up(y, d, NY), z, x, c) for d in range(1, NY)]
    barrier = pltpu.get_barrier_semaphore()
    for p in peers:
        pl.semaphore_signal(barrier, inc=1, device_id=p, device_id_type=MESH)
    icopy = pltpu.make_async_copy(ids, idv, isem)
    icopy.start()
    qcopy = pltpu.make_async_copy(query, qall.at[y], qsem)
    qcopy.start()
    load = pltpu.make_async_copy(slab, slabv, lsem)
    load.start()

    icopy.wait()
    wide = jnp.concatenate([idv[...]] * 8, axis=1)
    sub = lax.broadcasted_iota(jnp.int32, (16, 128), 0)
    lan = lax.broadcasted_iota(jnp.int32, (16, 128), 1)
    wide = jnp.where(lan // 16 == sub % 8, wide, 0)
    row = [jnp.sum(wide[8 * i:8 * i + 8], axis=0, keepdims=True) for i in range(2)]
    big_r = lax.broadcasted_iota(jnp.int32, (128, 128), 0)
    big_c = lax.broadcasted_iota(jnp.int32, (128, 128), 1)

    def column(v):
        return jnp.broadcast_to(v, (128, 128)).T

    each = slab.shape[0]
    own = [v // each for v in row]
    own_t = [column(v) for v in own]
    rank = [jnp.sum(jnp.where((own_t[0] == own[0]) & (big_r < big_c), 1, 0), axis=0, keepdims=True),
            jnp.sum(jnp.where(own_t[0] == own[1], 1, 0), axis=0, keepdims=True)
            + jnp.sum(jnp.where((own_t[1] == own[1]) & (big_r < big_c), 1, 0), axis=0, keepdims=True)]
    code_t = [column((own[i] * 16 + rank[i]) * each + row[i] % each) for i in range(2)]
    for zz in range(NZ):
        tab[zz] = sum(jnp.sum(jnp.where(code_t[i] // each == big_c + 128 * zz, code_t[i] % each, 0), axis=0, keepdims=True)
                      for i in range(2))
    for i in range(2):
        o = own[i]
        pos[i] = (((o // 8) * NC + o % 2) * NX + (o // 2) % 4) * CAP + rank[i]
    pcopy = pltpu.make_async_copy(pos, psm, psem)
    pcopy.start()
    tmid[z] = tab[z]

    pl.semaphore_wait(barrier, len(peers))
    sends = []

    def remote(src, dst, ssem, rsem, target):
        cp = pltpu.make_async_remote_copy(src_ref=src, dst_ref=dst, send_sem=ssem, recv_sem=rsem,
                                          device_id=target, device_id_type=MESH)
        cp.start()
        sends.append(cp)
        return cp

    first = [remote(tab.at[up(z, d, NZ)], tmid.at[z], ts1.at[d - 1], tr1.at[d - 1], dev(y, up(z, d, NZ), x, c))
             for d in range(1, NZ)]
    qcopy.wait()
    qcopies = [remote(qall.at[y], qall.at[y], qs.at[d - 1], qr.at[d - 1], dev(up(y, d, NY), z, x, c)) for d in range(1, NY)]
    for cp in first:
        cp.wait_recv()
    second = []
    for k, (d, e) in enumerate(WIDE):
        second.append(remote(tmid, tfin.at[jx], ts2.at[k], tr2.at[k], dev(y, z, up(x, d, NX), up(c, e, NC))))
    tfin[jx] = tmid[...]
    for cp in second:
        cp.wait_recv()
    tcopy = pltpu.make_async_copy(tfin, tsm, tsem)
    tcopy.start()
    load.wait()
    pcopy.wait()
    tcopy.wait()

    def tile(ch, at):
        n, r0, kind = CHUNKS[ch]
        if kind == 0:
            return slabv[at, r0:r0 + n, 0:128]
        top = slabv[at, r0:r0 + n, 128:256]
        low = slabv[at, 8 + r0:8 + r0 + n, 128:256]
        left = lax.broadcasted_iota(jnp.int32, (n, 128), 1) < 64
        if kind == 1:
            return jnp.where(left, top, pltpu.roll(low, 64, 1))
        return jnp.where(left, pltpu.roll(top, 64, 1), low)

    def gather(ch):
        for d in range(4):
            z2, x2 = up(z, d, NZ), up(x, d, NX)
            to_a = mid_a[ch] if d == 0 else src_a[ch]
            to_b = mid_b[ch] if d == 0 else src_b[ch]

            def body(j, carry):
                for s in range(HALF):
                    to_a[z2, j, s] = tile(ch, tsm[j, z2, 0, jx * 16 + s])
                for s in range(HALF):
                    to_b[x2, j, s] = tile(ch, tsm[x2 * NC + j % NC, j // NC, 0, jx * 16 + HALF + s])
                return carry

            lax.fori_loop(0, 8, body, 0)

    def stage1(ch):
        gather(ch)
        cps = []
        for d in (1, 3, 2):
            z2, x2 = up(z, d, NZ), up(x, d, NX)
            cps.append(remote(src_a[ch].at[z2], mid_a[ch].at[z], s1s.at[ch, 0, d - 1], s1r.at[ch, 0, d - 1], dev(y, z2, x, c)))
            cps.append(remote(src_b[ch].at[x2], mid_b[ch].at[x], s1s.at[ch, 1, d - 1], s1r.at[ch, 1, d - 1], dev(y, z, x2, c)))
        return cps

    def stage2(ch, before):
        for cp in before:
            cp.wait_recv()
        cps = []
        for k, (d, e) in enumerate(WIDE):
            z2, x2, c2 = up(z, d, NZ), up(x, d, NX), up(c, e, NC)
            cps.append(remote(mid_a[ch].at[:, x2 * NC + c2], fin[ch].at[:, c, x, 0:HALF], s2s.at[ch, 0, k], s2r.at[ch, 0, k], dev(y, z, x2, c2)))
            cps.append(remote(mid_b[ch].at[:, z2 * NC + c2], fin[ch].at[z, c, :, HALF:CAP], s2s.at[ch, 1, k], s2r.at[ch, 1, k], dev(y, z2, x, c2)))
        for i in range(4):
            fin[ch][i, c, x, 0:HALF] = mid_a[ch][i, jx]
            fin[ch][z, c, i, HALF:CAP] = mid_b[ch][i, jz]
        return cps

    def pick(ch, y2, q, out):
        flat = fin[ch].reshape(NZ * NC * NX * CAP, CHUNKS[ch][0], 128)
        upper = y2 // 2
        base = (y2 % 2) * 64 + q * 16
        for u in range(16):
            out[q * 16 + u] = flat[psm[upper, 0, base + u]]

    def across(ch, before):
        for cp in before:
            cp.wait_recv()
        cps = []
        for d in (1, 3, 2, 0):
            y2 = up(y, d, NY)
            out = ysend[ch].at[d - 1] if d else cand[ch].at[y]

            def body(q, carry):
                pick(ch, y2, q, out)
                return carry

            lax.fori_loop(0, 4, body, 0)
            if d:
                cps.append(remote(out, cand[ch].at[y], ys.at[ch, d - 1], yr.at[ch, d - 1], dev(y2, z, x, c)))
        return cps

    def across_last(ch, before):
        for cp in before:
            cp.wait_recv()
        cps = []
        for q in range(4):
            for d in (1, 3, 2, 0):
                y2 = up(y, d, NY)
                out = ysend[ch].at[d - 1] if d else cand[ch].at[y]
                pick(ch, y2, q, out)
                if d:
                    mine = pl.ds(q * 16, 16)
                    cps.append(remote(out.at[mine], cand[ch].at[y, mine], zs.at[q, d - 1], zr.at[q, d - 1], dev(y2, z, x, c)))
        return cps

    def nt(a, b):
        return lax.dot_general(a, b, (((1,), (1,)), ((), ())), preferred_element_type=F32)

    left16 = lax.broadcasted_iota(jnp.int32, (16, 8, 128), 2) < 64

    def swap(v):
        return pltpu.roll(v, 64, v.ndim - 1)

    def operands(q, kind):
        mine = pl.ds(q * 16, 16)
        if kind == 0:
            return [jnp.stack([cand[0][yy, mine], cand[1][yy, mine]], axis=1).reshape(256, 128) for yy in range(NY)]
        out = []
        for yy in range(0, NY, 2):
            a, b = (jnp.concatenate([cand[2 * kind][t, mine], cand[2 * kind + 1][t, mine]], axis=1) for t in (yy, yy + 1))
            top = jnp.where(left16, a, swap(b))
            low = jnp.where(left16, swap(a), b)
            out.append(jnp.stack([top, low], axis=1).reshape(256, 128))
        return out

    def partial(q, kind):
        s2 = jnp.zeros((256, 128), F32)
        dd = jnp.zeros((256, 128), F32)
        g = jnp.zeros((256, 256), F32)
        xs = operands(q, kind)
        at = (0, 4, 6)[kind]
        for k in range(0, len(xs), 2):
            his, los = [], []
            for t in (k, k + 1):
                v = xs[t]
                s2 = s2 + v * v
                dd = dd + v * qrow[q, at + t:at + t + 1, :]
                hi = v.astype(jnp.bfloat16)
                his.append(hi)
                los.append((v - hi.astype(F32)).astype(jnp.bfloat16))
            hi = jnp.concatenate(his, axis=1)
            lo = jnp.concatenate(los, axis=1)
            g = g + (nt(hi, hi) + (nt(hi, lo) + nt(lo, hi)))
        return g, s2, dd

    def query_rows():
        row16 = lax.broadcasted_iota(jnp.int32, (16, 256), 0)
        left = lax.broadcasted_iota(jnp.int32, (1, 128), 1) < 64
        for q in range(4):
            rows = [jnp.sum(jnp.where(row16 == 4 * y + q, qall[yy], 0.0), axis=0, keepdims=True) for yy in range(NY)]
            for yy in range(NY):
                qrow[q, yy:yy + 1, :] = rows[yy][:, 0:128]
            far = [v[:, 128:256] for v in rows]
            for k in range(2):
                qrow[q, 4 + k:5 + k, :] = jnp.where(left, far[2 * k], swap(far[2 * k + 1]))
                qrow[q, 6 + k:7 + k, :] = jnp.where(left, swap(far[2 * k]), far[2 * k + 1])

    hop1, hop2, hop3 = {}, {}, {}
    for stage, ch, *more in STEPS:
        if stage == 1:
            hop1[ch] = stage1(ch)
            if ch == 1:
                for cp in qcopies:
                    cp.wait_recv()
                query_rows()
        elif stage == 2:
            hop2[ch] = stage2(ch, hop1[ch])
        elif stage == 3:
            hop3[ch] = (across_last if ch == NCH - 1 else across)(ch, hop2[ch])
        elif stage == "wait":
            for cp in hop3[ch]:
                cp.wait_recv()
        else:
            q = more[0]
            g, s2, dd = partial(q, ch)
            acc[q] = g if ch == 0 else acc[q] + g
            sq[q] = s2 if ch == 0 else sq[q] + s2
            dt[q] = dd if ch == 0 else dt[q] + dd
    for cp in hop3[NCH - 2]:
        cp.wait_recv()

    lane = lax.broadcasted_iota(jnp.int32, (256, 128), 1)
    outs = []
    for q in range(4):
        for cp in hop3[NCH - 1][3 * q:3 * q + 3]:
            cp.wait_recv()
        g, s2, dd = partial(q, 2)
        g = g + acc[q]
        rn = 1.0 / jnp.sqrt(jnp.sum(s2 + sq[q], axis=1, keepdims=True) + EPS)
        dots = jnp.sum(dd + dt[q], axis=1, keepdims=True)
        qv = qrow[q]
        qn = jnp.sqrt(jnp.sum(jnp.sum(qv * qv, axis=0, keepdims=True), axis=1, keepdims=True) + EPS)
        score = (scale * dots) * (rn / qn)
        flat = jnp.where(lane == 0, score, rn).T
        gsend[q] = g * flat[1:2, :]
        ssend[q] = flat[0:2, :]
        for d in (1, 3, 2):
            y2 = up(y, d, NY)
            outs.append(remote(gsend.at[q, pl.ds(y2 * 64, 64)], part_out.at[y * 4 + q], gs.at[q, d - 1], gr.at[q, d - 1], dev(y2, z, x, c)))
            outs.append(remote(ssend.at[q], vec_out.at[y * 4 + q], ss.at[q, d - 1], sr.at[q, d - 1], dev(y2, z, x, c)))
        part_out[y * 4 + q] = gsend[q, pl.ds(pl.multiple_of(y * 64, 64), 64)]
        vec_out[y * 4 + q] = ssend[q]
    for cp in outs:
        cp.wait_recv()
    for cp in sends:
        cp.wait_send()


def main_call(scale, ids, query, slab):
    dma = pltpu.SemaphoreType.DMA
    vm = pltpu.VMEM
    vmem = pl.BlockSpec(memory_space=pltpu.VMEM)
    anywhere = pl.BlockSpec(memory_space=pl.ANY)
    sizes = [n for n, _, _ in CHUNKS]
    return pl.pallas_call(
        functools.partial(main_kernel, scale),
        out_shape=(pltpu.VMEM((16, 64, 256), F32), pltpu.VMEM((16, 2, 256), F32)),
        in_specs=[anywhere, anywhere, anywhere],
        out_specs=(vmem, vmem),
        scratch_shapes=[
            vm(slab.shape, F32), vm((16, 16), jnp.int32), vm((NY, 16, 256), F32), vm((4, 8, 128), F32),
            vm((4, 1, 128), jnp.int32), vm((4, 1, 128), jnp.int32), vm((8, 4, 1, 128), jnp.int32),
            pltpu.SMEM((8, 4, 1, 128), jnp.int32), vm((2, 1, 128), jnp.int32), pltpu.SMEM((2, 1, 128), jnp.int32),
            *[vm((4, 8, HALF, n, 128), F32) for _ in range(4) for n in sizes],
            *[vm((NZ, NC, NX, CAP, n, 128), F32) for n in sizes],
            *[vm((3, 64, n, 128), F32) for n in sizes],
            *[vm((NY, 64, n, 128), F32) for n in sizes],
            vm((4, 256, 256), F32), vm((4, 256, 128), F32), vm((4, 256, 128), F32),
            vm((4, 256, 256), F32), vm((4, 2, 256), F32),
            dma(()), dma(()), dma(()), dma(()), dma(()), dma((3,)), dma((3,)), dma((7,)), dma((7,)),
            dma((NCH, 2, 3)), dma((NCH, 2, 3)), dma((NCH, 2, 7)), dma((NCH, 2, 7)),
            dma((NCH, 3)), dma((NCH, 3)), dma((4, 3)), dma((4, 3)), dma((3,)), dma((3,)),
            dma((4, 3)), dma((4, 3)), dma((4, 3)), dma((4, 3)),
        ],
        compiler_params=pltpu.CompilerParams(collective_id=0, has_side_effects=True, vmem_limit_bytes=58 * 2**20),
    )(ids, query, slab)


def per_device(slab, queries, block_ids):
    query_count, width_part = queries.shape
    full_width = width_part * lax.axis_size("pb")
    blocks_each = slab.shape[0] // BLOCK
    part, vec = main_call(math.sqrt(full_width), block_ids, queries, slab.reshape(blocks_each, BLOCK, width_part))
    own = lax.dynamic_slice_in_dim(vec, lax.axis_index("pb") * 64, 64, 2)
    scores = vec[:, 0]
    gram = part * own[:, 1][:, :, None]
    penalty = gram * jax.nn.sigmoid(scores[:, None, :] - own[:, 0][:, :, None])
    return (scores, gram, penalty)


def solution(mesh):
    return jax.shard_map(
        per_device,
        mesh=mesh,
        in_specs=(P("db", "pb"), P("db", "pb"), P("db", None)),
        out_specs=(P("db", None), P("db", "pb", None), P("db", "pb", None)),
        check_vma=False,
    )
```

time: 134 us -> 115 us (0.86)
  Pallas kernels: 122 us -> 113 us
  local copies, waits for them, and re-layouts: 7.39 us -> 0.13 us
  other arithmetic: 3.56 us -> 1.67 us
    pallas_call x1, Pallas kernels: 122 us -> 113 us  [main_call(): pl.pallas_call(functools.partial(main_kernel, scale), out_shape=(pltpu.VM...]
    unnamed x4 -> x3, local copies, waits for them, and re-layouts: 3.02 us -> 0.01 us
    reshape x4 -> x0, local copies, waits for them, and re-layouts: 2.97 us -> none  [the longest x2 1.56 us: per_device(): ids = block_ids.reshape(request_count)]
where the time goes in v2:
time: 115 us
  Pallas kernels  113 us (98%)
  other arithmetic  1.67 us (1%)
    pallas_call x1, Pallas kernels, main_call(): pl.pallas_call(functools.partial(main_kernel, scale), out_shape=(pltpu.VM...  113 us

profile of v2, /device:TPU:1, one launch (start us, length us, event | category | flops | bytes accessed | tf_op | source)
XLA Modules:
  0.0 115.3 jit_solution(8149586284068636730)
XLA Ops:
  0.6 112.8 %shard_map.58 = (f32[16,64,256]{2,1,0:T(8,128)S(1)}, f32[16,2,256]{2,1,0:T(2,128)S(1)}) custom-call(s32[16,16]{1,0:T(8,128)} %ids.1, f32[16,256]{1,0:T(8,128)} %query.1, f32[512,16,256]{2,1,0:T(8,128)} %bitcast.6), custom_call_target="tpu_custom_call" | custom-call | tf_op jit(solution)/shard_map/pallas_call | solution.py:307
  113.5 0.1 constant_dynamic-slice_fusion
  113.6 0.0 copy-start
  113.6 1.7 %divide_multiply_fusion = (f32[16,64,256]{2,1,0:T(8,128)}, f32[16,64,256]{2,1,0:T(8,128)}) fusion(f32[16,64]{1,0:T(8,128)S(1)} %bitcast.10, f32[16,256]{1,0:T(8,128)S(1)} %bitcast.7, f32[16,64,256]{2,1,0:T(8,128)S(1)} %get-tuple-element.6, f32[16,64]{1,0:T(8,128)S(1)} %bitcast.9), kind=kLoop, calls=%fused_computation | loop fusion | flops 1572864 | bytes 3170304 | tf_op jit(solution)/shard_map/mul | solution.py:339
  115.3 0.0 copy-done
  (2 shorter events, 0.0 us)
Async XLA Ops:
  113.6 1.7 %copy-start = (f32[16,1,256]{2,0,1:T(8,128)}, f32[16,1,256]{2,0,1:T(8,128)S(1)}, u32[]{:S(2)}) copy-start(f32[16,1,256]{2,0,1:T(8,128)S(1)} %copy.8) | copy-start | bytes 49156

commit v3 on v2

--- a/solution.py
+++ b/solution.py
@@ -15,18 +15,18 @@
 EPS = 1e-06
 MESH = pl.DeviceIdType.MESH
 F32 = jnp.float32
-CHUNKS = ((8, 0, 0), (8, 8, 0), (4, 0, 1), (4, 4, 1), (4, 0, 2), (4, 4, 2))
+CHUNKS = ((8, 0, 0), (8, 8, 0), (4, 0, 1), (4, 4, 1), (4, 0, 2), (2, 4, 2), (2, 6, 2))
 NCH = len(CHUNKS)
 STEPS = ((1, 0), (1, 1), (2, 0), (1, 2), (2, 1), (1, 3), (3, 0), (2, 2), (1, 4), (3, 1), (2, 3), (1, 5), (3, 2), ("wait", 0), ("wait", 1),
-         ("sum", 0, 0), ("sum", 0, 1), (2, 4), ("sum", 0, 2), ("sum", 0, 3), (3, 3), (2, 5), ("wait", 2), ("wait", 3),
-         ("sum", 1, 0), ("sum", 1, 1), ("sum", 1, 2), ("sum", 1, 3), (3, 4), (3, 5))
+         ("sum", 0, 0), ("sum", 0, 1), (2, 4), (1, 6), ("sum", 0, 2), ("sum", 0, 3), (3, 3), (2, 5), (3, 4), (2, 6), ("wait", 2), ("wait", 3),
+         ("sum", 1, 0), ("sum", 1, 1), ("sum", 1, 2), ("sum", 1, 3), (3, 5), (3, 6))
 WIDE = [(d, e) for d in range(4) for e in range(2) if (d, e) != (0, 0)]
 
 
 def main_kernel(scale, ids, query, slab, part_out, vec_out, slabv, idv, qall, qrow, tab, tmid, tfin, tsm, pos, psm, *rest):
     src_a, mid_a, src_b, mid_b, fin, ysend, cand = (rest[i * NCH:(i + 1) * NCH] for i in range(7))
     (acc, sq, dt, gsend, ssend,
-     lsem, isem, psem, tsem, qsem, ts1, tr1, ts2, tr2, s1s, s1r, s2s, s2r, ys, yr, zs, zr, qs, qr, gs, gr, ss, sr) = rest[7 * NCH:]
+     lsem, isem, psem, tsem, qsem, ts1, tr1, ts2, tr2, qs, qr, s1s, s1r, s2s, s2r, ys, yr, zr, gs, gr, ss, sr) = rest[7 * NCH:]
     y = lax.axis_index("pb")
     db = lax.axis_index("db")
     z, x, c = db // (NX * NC), (db // NC) % NX, db % NC
@@ -82,27 +82,30 @@
     tmid[z] = tab[z]
 
     pl.semaphore_wait(barrier, len(peers))
-    sends = []
-
-    def remote(src, dst, ssem, rsem, target):
-        cp = pltpu.make_async_remote_copy(src_ref=src, dst_ref=dst, send_sem=ssem, recv_sem=rsem,
-                                          device_id=target, device_id_type=MESH)
-        cp.start()
-        sends.append(cp)
-        return cp
-
-    first = [remote(tab.at[up(z, d, NZ)], tmid.at[z], ts1.at[d - 1], tr1.at[d - 1], dev(y, up(z, d, NZ), x, c))
-             for d in range(1, NZ)]
+
+    def copy(src, dst, ssem, rsem, target):
+        return pltpu.make_async_remote_copy(src_ref=src, dst_ref=dst, send_sem=ssem, recv_sem=rsem,
+                                            device_id=target, device_id_type=MESH)
+
+    def remote(*args):
+        copy(*args).start()
+
+    def arrived(view, sem):
+        copy(view, view, sem, sem, peers[0]).wait_recv()
+
+    def left(view, sem):
+        copy(view, view, sem, sem, peers[0]).wait_send()
+
+    for d in range(1, NZ):
+        remote(tab.at[up(z, d, NZ)], tmid.at[z], ts1, tr1, dev(y, up(z, d, NZ), x, c))
     qcopy.wait()
-    qcopies = [remote(qall.at[y], qall.at[y], qs.at[d - 1], qr.at[d - 1], dev(up(y, d, NY), z, x, c)) for d in range(1, NY)]
-    for cp in first:
-        cp.wait_recv()
-    second = []
-    for k, (d, e) in enumerate(WIDE):
-        second.append(remote(tmid, tfin.at[jx], ts2.at[k], tr2.at[k], dev(y, z, up(x, d, NX), up(c, e, NC))))
+    for d in range(1, NY):
+        remote(qall.at[y], qall.at[y], qs, qr, dev(up(y, d, NY), z, x, c))
+    arrived(tmid.at[0:3], tr1)
+    for d, e in WIDE:
+        remote(tmid, tfin.at[jx], ts2, tr2, dev(y, z, up(x, d, NX), up(c, e, NC)))
     tfin[jx] = tmid[...]
-    for cp in second:
-        cp.wait_recv()
+    arrived(tfin.at[0:7], tr2)
     tcopy = pltpu.make_async_copy(tfin, tsm, tsem)
     tcopy.start()
     load.wait()
@@ -137,25 +140,25 @@
 
     def stage1(ch):
         gather(ch)
-        cps = []
         for d in (1, 3, 2):
             z2, x2 = up(z, d, NZ), up(x, d, NX)
-            cps.append(remote(src_a[ch].at[z2], mid_a[ch].at[z], s1s.at[ch, 0, d - 1], s1r.at[ch, 0, d - 1], dev(y, z2, x, c)))
-            cps.append(remote(src_b[ch].at[x2], mid_b[ch].at[x], s1s.at[ch, 1, d - 1], s1r.at[ch, 1, d - 1], dev(y, z, x2, c)))
-        return cps
-
-    def stage2(ch, before):
-        for cp in before:
-            cp.wait_recv()
-        cps = []
-        for k, (d, e) in enumerate(WIDE):
+            remote(src_a[ch].at[z2], mid_a[ch].at[z], s1s, s1r.at[ch, 0], dev(y, z2, x, c))
+            remote(src_b[ch].at[x2], mid_b[ch].at[x], s1s, s1r.at[ch, 1], dev(y, z, x2, c))
+
+    def stage2(ch):
+        arrived(mid_a[ch].at[0:3], s1r.at[ch, 0])
+        arrived(mid_b[ch].at[0:3], s1r.at[ch, 1])
+        for d, e in WIDE:
             z2, x2, c2 = up(z, d, NZ), up(x, d, NX), up(c, e, NC)
-            cps.append(remote(mid_a[ch].at[:, x2 * NC + c2], fin[ch].at[:, c, x, 0:HALF], s2s.at[ch, 0, k], s2r.at[ch, 0, k], dev(y, z, x2, c2)))
-            cps.append(remote(mid_b[ch].at[:, z2 * NC + c2], fin[ch].at[z, c, :, HALF:CAP], s2s.at[ch, 1, k], s2r.at[ch, 1, k], dev(y, z2, x, c2)))
+            remote(mid_a[ch].at[:, x2 * NC + c2], fin[ch].at[:, c, x, 0:HALF], s2s, s2r.at[ch, 0], dev(y, z, x2, c2))
+            remote(mid_b[ch].at[:, z2 * NC + c2], fin[ch].at[z, c, :, HALF:CAP], s2s, s2r.at[ch, 1], dev(y, z2, x, c2))
         for i in range(4):
             fin[ch][i, c, x, 0:HALF] = mid_a[ch][i, jx]
             fin[ch][z, c, i, HALF:CAP] = mid_b[ch][i, jz]
-        return cps
+
+    def both_arrived(ch):
+        arrived(mid_a[ch].at[:, 0:7], s2r.at[ch, 0])
+        arrived(mid_b[ch].at[:, 0:7], s2r.at[ch, 1])
 
     def pick(ch, y2, q, out):
         flat = fin[ch].reshape(NZ * NC * NX * CAP, CHUNKS[ch][0], 128)
@@ -164,10 +167,8 @@
         for u in range(16):
             out[q * 16 + u] = flat[psm[upper, 0, base + u]]
 
-    def across(ch, before):
-        for cp in before:
-            cp.wait_recv()
-        cps = []
+    def across(ch):
+        both_arrived(ch)
         for d in (1, 3, 2, 0):
             y2 = up(y, d, NY)
             out = ysend[ch].at[d - 1] if d else cand[ch].at[y]
@@ -178,22 +179,18 @@
 
             lax.fori_loop(0, 4, body, 0)
             if d:
-                cps.append(remote(out, cand[ch].at[y], ys.at[ch, d - 1], yr.at[ch, d - 1], dev(y2, z, x, c)))
-        return cps
-
-    def across_last(ch, before):
-        for cp in before:
-            cp.wait_recv()
-        cps = []
+                remote(out, cand[ch].at[y], ys, yr.at[ch], dev(y2, z, x, c))
+
+    def across_last(ch):
+        both_arrived(ch)
         for q in range(4):
+            mine = pl.ds(q * 16, 16)
             for d in (1, 3, 2, 0):
                 y2 = up(y, d, NY)
                 out = ysend[ch].at[d - 1] if d else cand[ch].at[y]
                 pick(ch, y2, q, out)
                 if d:
-                    mine = pl.ds(q * 16, 16)
-                    cps.append(remote(out.at[mine], cand[ch].at[y, mine], zs.at[q, d - 1], zr.at[q, d - 1], dev(y2, z, x, c)))
-        return cps
+                    remote(out.at[mine], cand[ch].at[y, mine], ys, zr.at[q], dev(y2, z, x, c))
 
     def nt(a, b):
         return lax.dot_general(a, b, (((1,), (1,)), ((), ())), preferred_element_type=F32)
@@ -209,7 +206,7 @@
             return [jnp.stack([cand[0][yy, mine], cand[1][yy, mine]], axis=1).reshape(256, 128) for yy in range(NY)]
         out = []
         for yy in range(0, NY, 2):
-            a, b = (jnp.concatenate([cand[2 * kind][t, mine], cand[2 * kind + 1][t, mine]], axis=1) for t in (yy, yy + 1))
+            a, b = (jnp.concatenate([cand[ch][t, mine] for ch in range(NCH) if CHUNKS[ch][2] == kind], axis=1) for t in (yy, yy + 1))
             top = jnp.where(left16, a, swap(b))
             low = jnp.where(left16, swap(a), b)
             out.append(jnp.stack([top, low], axis=1).reshape(256, 128))
@@ -247,35 +244,31 @@
                 qrow[q, 4 + k:5 + k, :] = jnp.where(left, far[2 * k], swap(far[2 * k + 1]))
                 qrow[q, 6 + k:7 + k, :] = jnp.where(left, swap(far[2 * k]), far[2 * k + 1])
 
-    hop1, hop2, hop3 = {}, {}, {}
     for stage, ch, *more in STEPS:
         if stage == 1:
-            hop1[ch] = stage1(ch)
+            stage1(ch)
             if ch == 1:
-                for cp in qcopies:
-                    cp.wait_recv()
+                arrived(qall.at[0:3], qr)
                 query_rows()
         elif stage == 2:
-            hop2[ch] = stage2(ch, hop1[ch])
+            stage2(ch)
         elif stage == 3:
-            hop3[ch] = (across_last if ch == NCH - 1 else across)(ch, hop2[ch])
+            (across_last if ch == NCH - 1 else across)(ch)
         elif stage == "wait":
-            for cp in hop3[ch]:
-                cp.wait_recv()
+            arrived(cand[ch].at[0:3], yr.at[ch])
         else:
             q = more[0]
             g, s2, dd = partial(q, ch)
             acc[q] = g if ch == 0 else acc[q] + g
             sq[q] = s2 if ch == 0 else sq[q] + s2
             dt[q] = dd if ch == 0 else dt[q] + dd
-    for cp in hop3[NCH - 2]:
-        cp.wait_recv()
+    for ch in range(NCH - 1):
+        if CHUNKS[ch][2] == 2:
+            arrived(cand[ch].at[0:3], yr.at[ch])
 
     lane = lax.broadcasted_iota(jnp.int32, (256, 128), 1)
-    outs = []
     for q in range(4):
-        for cp in hop3[NCH - 1][3 * q:3 * q + 3]:
-            cp.wait_recv()
+        arrived(cand[NCH - 1].at[0:3, pl.ds(q * 16, 16)], zr.at[q])
         g, s2, dd = partial(q, 2)
         g = g + acc[q]
         rn = 1.0 / jnp.sqrt(jnp.sum(s2 + sq[q], axis=1, keepdims=True) + EPS)
@@ -288,14 +281,20 @@
         ssend[q] = flat[0:2, :]
         for d in (1, 3, 2):
             y2 = up(y, d, NY)
-            outs.append(remote(gsend.at[q, pl.ds(y2 * 64, 64)], part_out.at[y * 4 + q], gs.at[q, d - 1], gr.at[q, d - 1], dev(y2, z, x, c)))
-            outs.append(remote(ssend.at[q], vec_out.at[y * 4 + q], ss.at[q, d - 1], sr.at[q, d - 1], dev(y2, z, x, c)))
+            remote(gsend.at[q, pl.ds(y2 * 64, 64)], part_out.at[y * 4 + q], gs, gr, dev(y2, z, x, c))
+            remote(ssend.at[q], vec_out.at[y * 4 + q], ss, sr, dev(y2, z, x, c))
         part_out[y * 4 + q] = gsend[q, pl.ds(pl.multiple_of(y * 64, 64), 64)]
         vec_out[y * 4 + q] = ssend[q]
-    for cp in outs:
-        cp.wait_recv()
-    for cp in sends:
-        cp.wait_send()
+    arrived(part_out.at[0:12], gr)
+    arrived(vec_out.at[0:12], sr)
+    left(part_out.at[0:12], gs)
+    left(vec_out.at[0:12], ss)
+    left(tmid.at[0:3], ts1)
+    left(tfin.at[0:7], ts2)
+    left(qall.at[0:3], qs)
+    left(slabv.at[0:288], s1s)
+    left(slabv.at[0:336], s2s)
+    left(slabv.at[0:192], ys)
 
 
 def main_call(scale, ids, query, slab):
@@ -319,10 +318,7 @@
             *[vm((NY, 64, n, 128), F32) for n in sizes],
             vm((4, 256, 256), F32), vm((4, 256, 128), F32), vm((4, 256, 128), F32),
             vm((4, 256, 256), F32), vm((4, 2, 256), F32),
-            dma(()), dma(()), dma(()), dma(()), dma(()), dma((3,)), dma((3,)), dma((7,)), dma((7,)),
-            dma((NCH, 2, 3)), dma((NCH, 2, 3)), dma((NCH, 2, 7)), dma((NCH, 2, 7)),
-            dma((NCH, 3)), dma((NCH, 3)), dma((4, 3)), dma((4, 3)), dma((3,)), dma((3,)),
-            dma((4, 3)), dma((4, 3)), dma((4, 3)), dma((4, 3)),
+            *[dma(()) for _ in range(12)], dma((NCH, 2)), dma(()), dma((NCH, 2)), dma(()), dma((NCH,)), dma((4,)), *[dma(()) for _ in range(4)],
         ],
         compiler_params=pltpu.CompilerParams(collective_id=0, has_side_effects=True, vmem_limit_bytes=58 * 2**20),
     )(ids, query, slab)

time: 115 us -> 112 us (0.974)
  Pallas kernels: 113 us -> 109 us
    pallas_call x1, Pallas kernels: 113 us -> 109 us  [main_call(): pl.pallas_call(functools.partial(main_kernel, scale), out_shape=(pltpu.VM...]
where the time goes in v3:
time: 112 us
  Pallas kernels  109 us (97%)
  other arithmetic  1.67 us (1%)
    pallas_call x1, Pallas kernels, main_call(): pl.pallas_call(functools.partial(main_kernel, scale), out_shape=(pltpu.VM...  109 us

profile of v3, /device:TPU:1, one launch (start us, length us, event | category | flops | bytes accessed | tf_op | source)
XLA Modules:
  0.0 111.9 jit_solution(11054681865838229463)
XLA Ops:
  0.6 109.4 %shard_map.58 = (f32[16,64,256]{2,1,0:T(8,128)S(1)}, f32[16,2,256]{2,1,0:T(2,128)S(1)}) custom-call(s32[16,16]{1,0:T(8,128)} %ids.1, f32[16,256]{1,0:T(8,128)} %query.1, f32[512,16,256]{2,1,0:T(8,128)} %bitcast.6), custom_call_target="tpu_custom_call" | custom-call | tf_op jit(solution)/shard_map/pallas_call | solution.py:306
  110.1 0.1 constant_dynamic-slice_fusion
  110.2 0.0 copy-start
  110.2 1.7 %divide_multiply_fusion = (f32[16,64,256]{2,1,0:T(8,128)}, f32[16,64,256]{2,1,0:T(8,128)}) fusion(f32[16,64]{1,0:T(8,128)S(1)} %bitcast.10, f32[16,256]{1,0:T(8,128)S(1)} %bitcast.7, f32[16,64,256]{2,1,0:T(8,128)S(1)} %get-tuple-element.6, f32[16,64]{1,0:T(8,128)S(1)} %bitcast.9), kind=kLoop, calls=%fused_computation | loop fusion | flops 1572864 | bytes 3170304 | tf_op jit(solution)/shard_map/mul | solution.py:335
  111.9 0.0 copy-done
  (2 shorter events, 0.0 us)
Async XLA Ops:
  110.2 1.7 %copy-start = (f32[16,1,256]{2,0,1:T(8,128)}, f32[16,1,256]{2,0,1:T(8,128)S(1)}, u32[]{:S(2)}) copy-start(f32[16,1,256]{2,0,1:T(8,128)S(1)} %copy.8) | copy-start | bytes 49156

commit v4 on v3

--- a/solution.py
+++ b/solution.py
@@ -15,18 +15,18 @@
 EPS = 1e-06
 MESH = pl.DeviceIdType.MESH
 F32 = jnp.float32
-CHUNKS = ((8, 0, 0), (8, 8, 0), (4, 0, 1), (4, 4, 1), (4, 0, 2), (2, 4, 2), (2, 6, 2))
+CHUNKS = ((8, 0, 0), (8, 8, 0), (4, 0, 1), (4, 4, 1), (2, 0, 2), (2, 2, 2), (2, 4, 2), (2, 6, 2))
 NCH = len(CHUNKS)
-STEPS = ((1, 0), (1, 1), (2, 0), (1, 2), (2, 1), (1, 3), (3, 0), (2, 2), (1, 4), (3, 1), (2, 3), (1, 5), (3, 2), ("wait", 0), ("wait", 1),
-         ("sum", 0, 0), ("sum", 0, 1), (2, 4), (1, 6), ("sum", 0, 2), ("sum", 0, 3), (3, 3), (2, 5), (3, 4), (2, 6), ("wait", 2), ("wait", 3),
-         ("sum", 1, 0), ("sum", 1, 1), ("sum", 1, 2), ("sum", 1, 3), (3, 5), (3, 6))
+STEPS = ((1, 1), (2, 0), (1, 2), (2, 1), (1, 3), (3, 0), (2, 2), (1, 4), (3, 1), (2, 3), (1, 5), ("wait", 0), (3, 2), ("wait", 1),
+         ("sum", 0, 0), ("sum", 0, 1), (2, 4), (1, 6), ("sum", 0, 2), (3, 3), ("sum", 0, 3), (2, 5), (1, 7), (3, 4), (2, 6), (3, 5), (2, 7),
+         ("wait", 2), ("wait", 3), ("sum", 1, 0), ("sum", 1, 1), ("sum", 1, 2), ("sum", 1, 3), (3, 6), (3, 7))
 WIDE = [(d, e) for d in range(4) for e in range(2) if (d, e) != (0, 0)]
 
 
-def main_kernel(scale, ids, query, slab, part_out, vec_out, slabv, idv, qall, qrow, tab, tmid, tfin, tsm, pos, psm, *rest):
+def main_kernel(scale, ids, query, slab, part_out, vec_out, slabv, idv, qall, qrow, tab, near, far, nsm, fsm, pos, psm, *rest):
     src_a, mid_a, src_b, mid_b, fin, ysend, cand = (rest[i * NCH:(i + 1) * NCH] for i in range(7))
     (acc, sq, dt, gsend, ssend,
-     lsem, isem, psem, tsem, qsem, ts1, tr1, ts2, tr2, qs, qr, s1s, s1r, s2s, s2r, ys, yr, zr, gs, gr, ss, sr) = rest[7 * NCH:]
+     lsem, isem, psem, nsem, fsem, qsem, ts1, tr1, ts2, tr2, qs, qr, s1s, s1r, s2s, s2r, ys, yr, zr, gs, gr, ss, sr) = rest[7 * NCH:]
     y = lax.axis_index("pb")
     db = lax.axis_index("db")
     z, x, c = db // (NX * NC), (db // NC) % NX, db % NC
@@ -79,7 +79,9 @@
         pos[i] = (((o // 8) * NC + o % 2) * NX + (o // 2) % 4) * CAP + rank[i]
     pcopy = pltpu.make_async_copy(pos, psm, psem)
     pcopy.start()
-    tmid[z] = tab[z]
+    near[z * NC + c] = tab[z]
+    near[8 + jx] = tab[z]
+    near[8 + x * NC + 1 - c] = tab[z]
 
     pl.semaphore_wait(barrier, len(peers))
 
@@ -96,21 +98,20 @@
     def left(view, sem):
         copy(view, view, sem, sem, peers[0]).wait_send()
 
-    for d in range(1, NZ):
-        remote(tab.at[up(z, d, NZ)], tmid.at[z], ts1, tr1, dev(y, up(z, d, NZ), x, c))
-    qcopy.wait()
-    for d in range(1, NY):
-        remote(qall.at[y], qall.at[y], qs, qr, dev(up(y, d, NY), z, x, c))
-    arrived(tmid.at[0:3], tr1)
     for d, e in WIDE:
-        remote(tmid, tfin.at[jx], ts2, tr2, dev(y, z, up(x, d, NX), up(c, e, NC)))
-    tfin[jx] = tmid[...]
-    arrived(tfin.at[0:7], tr2)
-    tcopy = pltpu.make_async_copy(tfin, tsm, tsem)
-    tcopy.start()
+        z2, c2 = up(z, d, NZ), up(c, e, NC)
+        remote(tab.at[z2], near.at[z * NC + c], ts1, tr1, dev(y, z2, x, c2))
+        if d:
+            x2 = up(x, d, NX)
+            remote(tab.at[z], near.at[8 + jx], ts1, tr1, dev(y, z, x2, c2))
+    arrived(near.at[0:13], tr1)
+    ncopy = pltpu.make_async_copy(near, nsm, nsem)
+    ncopy.start()
+    for d in range(1, NX):
+        remote(near.at[0:8], far.at[x], ts2, tr2, dev(y, z, up(x, d, NX), c))
+    far[x] = near[0:8]
     load.wait()
-    pcopy.wait()
-    tcopy.wait()
+    ncopy.wait()
 
     def tile(ch, at):
         n, r0, kind = CHUNKS[ch]
@@ -123,20 +124,63 @@
             return jnp.where(left, top, pltpu.roll(low, 64, 1))
         return jnp.where(left, pltpu.roll(top, 64, 1), low)
 
+    def fill(ch, to, at, row, first):
+        for s in range(HALF):
+            to[ch][(*at, s)] = tile(ch, row(jx * 16 + first + s))
+
     def gather(ch):
         for d in range(4):
             z2, x2 = up(z, d, NZ), up(x, d, NX)
-            to_a = mid_a[ch] if d == 0 else src_a[ch]
-            to_b = mid_b[ch] if d == 0 else src_b[ch]
 
             def body(j, carry):
-                for s in range(HALF):
-                    to_a[z2, j, s] = tile(ch, tsm[j, z2, 0, jx * 16 + s])
-                for s in range(HALF):
-                    to_b[x2, j, s] = tile(ch, tsm[x2 * NC + j % NC, j // NC, 0, jx * 16 + HALF + s])
+                fill(ch, src_a if d else mid_a, (z2, j), lambda k: fsm[j // NC, z2 * NC + j % NC, 0, k], 0)
+                fill(ch, src_b if d else mid_b, (x2, j), lambda k: fsm[x2, j, 0, k], HALF)
                 return carry
 
             lax.fori_loop(0, 8, body, 0)
+
+    def open_near():
+        for d in range(4):
+            z2, x2 = up(z, d, NZ), up(x, d, NX)
+            line = (8 + x2 * NC) if d else z * NC
+
+            def body(e, carry):
+                if d:
+                    fill(0, src_a, (z2, x * NC + e), lambda k: nsm[z2 * NC + e, 0, k], 0)
+                    fill(0, src_b, (x2, z * NC + e), lambda k: nsm[line + e, 0, k], HALF)
+                fill(0, mid_a, (z, x2 * NC + e), lambda k: nsm[line + e, 0, k], 0)
+                fill(0, mid_b, (x, z2 * NC + e), lambda k: nsm[z2 * NC + e, 0, k], HALF)
+                return carry
+
+            lax.fori_loop(0, 2, body, 0)
+        for d in (1, 3, 2):
+            z2, x2 = up(z, d, NZ), up(x, d, NX)
+            mine_a, mine_b = pl.ds(x * NC, NC), pl.ds(z * NC, NC)
+            remote(src_a[0].at[z2, mine_a], mid_a[0].at[z, mine_a], s1s, s1r.at[0, 0], dev(y, z2, x, c))
+            remote(src_b[0].at[x2, mine_b], mid_b[0].at[x, mine_b], s1s, s1r.at[0, 1], dev(y, z, x2, c))
+        for d, e in WIDE:
+            z2, x2, c2 = up(z, d, NZ), up(x, d, NX), up(c, e, NC)
+            remote(mid_a[0].at[z, x2 * NC + c2], fin[0].at[z, c, x, 0:HALF], s2s, s2r.at[0, 0], dev(y, z, x2, c2))
+            remote(mid_b[0].at[x, z2 * NC + c2], fin[0].at[z, c, x, HALF:CAP], s2s, s2r.at[0, 1], dev(y, z2, x, c2))
+
+    def open_far():
+        for d in range(1, 4):
+            z2, x2 = up(z, d, NZ), up(x, d, NX)
+
+            def body(i, carry):
+                k2, e = up(i // NC, 1, 4), i % NC
+                z3, x3 = up(z, k2, NZ), up(x, k2, NX)
+                fill(0, src_a, (z2, x3 * NC + e), lambda k: fsm[x3, z2 * NC + e, 0, k], 0)
+                fill(0, src_b, (x2, z3 * NC + e), lambda k: fsm[x2, z3 * NC + e, 0, k], HALF)
+                return carry
+
+            lax.fori_loop(0, 6, body, 0)
+        for d in (1, 3, 2):
+            for k2 in range(1, 4):
+                z2, x2 = up(z, d, NZ), up(x, d, NX)
+                their_a, their_b = pl.ds(up(x, k2, NX) * NC, NC), pl.ds(up(z, k2, NZ) * NC, NC)
+                remote(src_a[0].at[z2, their_a], mid_a[0].at[z, their_a], s1s, s1r.at[0, 0], dev(y, z2, x, c))
+                remote(src_b[0].at[x2, their_b], mid_b[0].at[x, their_b], s1s, s1r.at[0, 1], dev(y, z, x2, c))
 
     def stage1(ch):
         gather(ch)
@@ -150,8 +194,14 @@
         arrived(mid_b[ch].at[0:3], s1r.at[ch, 1])
         for d, e in WIDE:
             z2, x2, c2 = up(z, d, NZ), up(x, d, NX), up(c, e, NC)
-            remote(mid_a[ch].at[:, x2 * NC + c2], fin[ch].at[:, c, x, 0:HALF], s2s, s2r.at[ch, 0], dev(y, z, x2, c2))
-            remote(mid_b[ch].at[:, z2 * NC + c2], fin[ch].at[z, c, :, HALF:CAP], s2s, s2r.at[ch, 1], dev(y, z2, x, c2))
+            if ch:
+                remote(mid_a[ch].at[:, x2 * NC + c2], fin[ch].at[:, c, x, 0:HALF], s2s, s2r.at[ch, 0], dev(y, z, x2, c2))
+                remote(mid_b[ch].at[:, z2 * NC + c2], fin[ch].at[z, c, :, HALF:CAP], s2s, s2r.at[ch, 1], dev(y, z2, x, c2))
+            else:
+                for k2 in range(1, 4):
+                    z3, x3 = up(z, k2, NZ), up(x, k2, NX)
+                    remote(mid_a[0].at[z3, x2 * NC + c2], fin[0].at[z3, c, x, 0:HALF], s2s, s2r.at[0, 0], dev(y, z, x2, c2))
+                    remote(mid_b[0].at[x3, z2 * NC + c2], fin[0].at[z, c, x3, HALF:CAP], s2s, s2r.at[0, 1], dev(y, z2, x, c2))
         for i in range(4):
             fin[ch][i, c, x, 0:HALF] = mid_a[ch][i, jx]
             fin[ch][z, c, i, HALF:CAP] = mid_b[ch][i, jz]
@@ -244,6 +294,16 @@
                 qrow[q, 4 + k:5 + k, :] = jnp.where(left, far[2 * k], swap(far[2 * k + 1]))
                 qrow[q, 6 + k:7 + k, :] = jnp.where(left, swap(far[2 * k]), far[2 * k + 1])
 
+    open_near()
+    arrived(far.at[0:3], tr2)
+    fcopy = pltpu.make_async_copy(far, fsm, fsem)
+    fcopy.start()
+    qcopy.wait()
+    for d in range(1, NY):
+        remote(qall.at[y], qall.at[y], qs, qr, dev(up(y, d, NY), z, x, c))
+    fcopy.wait()
+    open_far()
+    pcopy.wait()
     for stage, ch, *more in STEPS:
         if stage == 1:
             stage1(ch)
@@ -289,8 +349,8 @@
     arrived(vec_out.at[0:12], sr)
     left(part_out.at[0:12], gs)
     left(vec_out.at[0:12], ss)
-    left(tmid.at[0:3], ts1)
-    left(tfin.at[0:7], ts2)
+    left(near.at[0:13], ts1)
+    left(far.at[0:3], ts2)
     left(qall.at[0:3], qs)
     left(slabv.at[0:288], s1s)
     left(slabv.at[0:336], s2s)
@@ -310,15 +370,15 @@
         out_specs=(vmem, vmem),
         scratch_shapes=[
             vm(slab.shape, F32), vm((16, 16), jnp.int32), vm((NY, 16, 256), F32), vm((4, 8, 128), F32),
-            vm((4, 1, 128), jnp.int32), vm((4, 1, 128), jnp.int32), vm((8, 4, 1, 128), jnp.int32),
-            pltpu.SMEM((8, 4, 1, 128), jnp.int32), vm((2, 1, 128), jnp.int32), pltpu.SMEM((2, 1, 128), jnp.int32),
+            vm((4, 1, 128), jnp.int32), vm((16, 1, 128), jnp.int32), vm((4, 8, 1, 128), jnp.int32),
+            pltpu.SMEM((16, 1, 128), jnp.int32), pltpu.SMEM((4, 8, 1, 128), jnp.int32), vm((2, 1, 128), jnp.int32), pltpu.SMEM((2, 1, 128), jnp.int32),
             *[vm((4, 8, HALF, n, 128), F32) for _ in range(4) for n in sizes],
             *[vm((NZ, NC, NX, CAP, n, 128), F32) for n in sizes],
             *[vm((3, 64, n, 128), F32) for n in sizes],
             *[vm((NY, 64, n, 128), F32) for n in sizes],
             vm((4, 256, 256), F32), vm((4, 256, 128), F32), vm((4, 256, 128), F32),
             vm((4, 256, 256), F32), vm((4, 2, 256), F32),
-            *[dma(()) for _ in range(12)], dma((NCH, 2)), dma(()), dma((NCH, 2)), dma(()), dma((NCH,)), dma((4,)), *[dma(()) for _ in range(4)],
+            *[dma(()) for _ in range(13)], dma((NCH, 2)), dma(()), dma((NCH, 2)), dma(()), dma((NCH,)), dma((4,)), *[dma(()) for _ in range(4)],
         ],
         compiler_params=pltpu.CompilerParams(collective_id=0, has_side_effects=True, vmem_limit_bytes=58 * 2**20),
     )(ids, query, slab)

time: 112 us -> 105 us (0.938)
  Pallas kernels: 109 us -> 102 us
    pallas_call x1, Pallas kernels: 109 us -> 102 us  [main_call(): pl.pallas_call(functools.partial(main_kernel, scale), out_shape=(pltpu.VM...]
where the time goes in v4:
time: 105 us; the launch traced here: 104 us
  Pallas kernels  102 us (97%)
  other arithmetic  1.67 us (2%)
    pallas_call x1, Pallas kernels, main_call(): pl.pallas_call(functools.partial(main_kernel, scale), out_shape=(pltpu.VM...  102 us

profile of v4, /device:TPU:1, one launch (start us, length us, event | category | flops | bytes accessed | tf_op | source)
XLA Modules:
  0.0 104.5 jit_solution(15318624756666322812)
XLA Ops:
  0.6 102.0 %shard_map.58 = (f32[16,64,256]{2,1,0:T(8,128)S(1)}, f32[16,2,256]{2,1,0:T(2,128)S(1)}) custom-call(s32[16,16]{1,0:T(8,128)} %ids.1, f32[16,256]{1,0:T(8,128)} %query.1, f32[512,16,256]{2,1,0:T(8,128)} %bitcast.6), custom_call_target="tpu_custom_call" | custom-call | tf_op jit(solution)/shard_map/pallas_call | solution.py:366
  102.6 0.1 constant_dynamic-slice_fusion
  102.8 0.0 copy-start
  102.8 1.7 %divide_multiply_fusion = (f32[16,64,256]{2,1,0:T(8,128)}, f32[16,64,256]{2,1,0:T(8,128)}) fusion(f32[16,64]{1,0:T(8,128)S(1)} %bitcast.10, f32[16,256]{1,0:T(8,128)S(1)} %bitcast.7, f32[16,64,256]{2,1,0:T(8,128)S(1)} %get-tuple-element.6, f32[16,64]{1,0:T(8,128)S(1)} %bitcast.9), kind=kLoop, calls=%fused_computation | loop fusion | flops 1572864 | bytes 3170304 | tf_op jit(solution)/shard_map/mul | solution.py:395
  104.5 0.0 copy-done
  (2 shorter events, 0.0 us)
Async XLA Ops:
  102.8 1.7 %copy-start = (f32[16,1,256]{2,0,1:T(8,128)}, f32[16,1,256]{2,0,1:T(8,128)S(1)}, u32[]{:S(2)}) copy-start(f32[16,1,256]{2,0,1:T(8,128)S(1)} %copy.8) | copy-start | bytes 49156

commit v5 on v4

--- a/solution.py
+++ b/solution.py
@@ -17,10 +17,11 @@
 F32 = jnp.float32
 CHUNKS = ((8, 0, 0), (8, 8, 0), (4, 0, 1), (4, 4, 1), (2, 0, 2), (2, 2, 2), (2, 4, 2), (2, 6, 2))
 NCH = len(CHUNKS)
-STEPS = ((1, 1), (2, 0), (1, 2), (2, 1), (1, 3), (3, 0), (2, 2), (1, 4), (3, 1), (2, 3), (1, 5), ("wait", 0), (3, 2), ("wait", 1),
-         ("sum", 0, 0), ("sum", 0, 1), (2, 4), (1, 6), ("sum", 0, 2), (3, 3), ("sum", 0, 3), (2, 5), (1, 7), (3, 4), (2, 6), (3, 5), (2, 7),
-         ("wait", 2), ("wait", 3), ("sum", 1, 0), ("sum", 1, 1), ("sum", 1, 2), ("sum", 1, 3), (3, 6), (3, 7))
-WIDE = [(d, e) for d in range(4) for e in range(2) if (d, e) != (0, 0)]
+STEPS = ((1, 1), (2, 0), (1, 2), (2, 1), (1, 3), (3, 0), (2, 2), (1, 4), (3, 1), ("wait", 0), (2, 3), (1, 5), (3, 2), (2, 4), (1, 6), ("wait", 1),
+         ("sum", 0, 0), ("sum", 0, 1), (3, 3), (2, 5), (1, 7), ("sum", 0, 2), (3, 4), (2, 6), ("sum", 0, 3), ("wait", 2), ("wait", 3), (3, 5),
+         (2, 7), ("sum", 1, 0), ("sum", 1, 1), (3, 6), ("sum", 1, 2), ("sum", 1, 3), (3, 7))
+FAR = (1, 3, 2)
+WIDE = ((1, 0), (3, 0), (1, 1), (3, 1), (2, 0), (2, 1), (0, 1))
 
 
 def main_kernel(scale, ids, query, slab, part_out, vec_out, slabv, idv, qall, qrow, tab, near, far, nsm, fsm, pos, psm, *rest):
@@ -39,9 +40,9 @@
     def up(v, d, n):
         return (v + d) % n
 
-    peers = [dev(y, up(z, d, NZ), x, up(c, e, NC)) for d, e in WIDE]
-    peers += [dev(y, z, up(x, d, NX), up(c, e, NC)) for d, e in WIDE if d]
-    peers += [dev(up(y, d, NY), z, x, c) for d in range(1, NY)]
+    peers = [dev(y, *at, up(c, e, NC)) for d, e in WIDE if d for at in ((up(z, d, NZ), x), (z, up(x, d, NX)))]
+    peers[4:4] = [dev(up(y, d, NY), z, x, c) for d in FAR]
+    peers.append(dev(y, z, x, up(c, 1, NC)))
     barrier = pltpu.get_barrier_semaphore()
     for p in peers:
         pl.semaphore_signal(barrier, inc=1, device_id=p, device_id_type=MESH)
@@ -107,7 +108,7 @@
     arrived(near.at[0:13], tr1)
     ncopy = pltpu.make_async_copy(near, nsm, nsem)
     ncopy.start()
-    for d in range(1, NX):
+    for d in FAR:
         remote(near.at[0:8], far.at[x], ts2, tr2, dev(y, z, up(x, d, NX), c))
     far[x] = near[0:8]
     load.wait()
@@ -153,7 +154,7 @@
                 return carry
 
             lax.fori_loop(0, 2, body, 0)
-        for d in (1, 3, 2):
+        for d in FAR:
             z2, x2 = up(z, d, NZ), up(x, d, NX)
             mine_a, mine_b = pl.ds(x * NC, NC), pl.ds(z * NC, NC)
             remote(src_a[0].at[z2, mine_a], mid_a[0].at[z, mine_a], s1s, s1r.at[0, 0], dev(y, z2, x, c))
@@ -175,7 +176,7 @@
                 return carry
 
             lax.fori_loop(0, 6, body, 0)
-        for d in (1, 3, 2):
+        for d in FAR:
             for k2 in range(1, 4):
                 z2, x2 = up(z, d, NZ), up(x, d, NX)
                 their_a, their_b = pl.ds(up(x, k2, NX) * NC, NC), pl.ds(up(z, k2, NZ) * NC, NC)
@@ -184,7 +185,7 @@
 
     def stage1(ch):
         gather(ch)
-        for d in (1, 3, 2):
+        for d in FAR:
             z2, x2 = up(z, d, NZ), up(x, d, NX)
             remote(src_a[ch].at[z2], mid_a[ch].at[z], s1s, s1r.at[ch, 0], dev(y, z2, x, c))
             remote(src_b[ch].at[x2], mid_b[ch].at[x], s1s, s1r.at[ch, 1], dev(y, z, x2, c))
@@ -219,7 +220,7 @@
 
     def across(ch):
         both_arrived(ch)
-        for d in (1, 3, 2, 0):
+        for d in (*FAR, 0):
             y2 = up(y, d, NY)
             out = ysend[ch].at[d - 1] if d else cand[ch].at[y]
 
@@ -235,7 +236,7 @@
         both_arrived(ch)
         for q in range(4):
             mine = pl.ds(q * 16, 16)
-            for d in (1, 3, 2, 0):
+            for d in (*FAR, 0):
                 y2 = up(y, d, NY)
                 out = ysend[ch].at[d - 1] if d else cand[ch].at[y]
                 pick(ch, y2, q, out)
@@ -331,19 +332,19 @@
         arrived(cand[NCH - 1].at[0:3, pl.ds(q * 16, 16)], zr.at[q])
         g, s2, dd = partial(q, 2)
         g = g + acc[q]
+        gsend[q] = g
+        for d in FAR:
+            y2 = up(y, d, NY)
+            remote(gsend.at[q, pl.ds(y2 * 64, 64)], part_out.at[y * 4 + q], gs, gr, dev(y2, z, x, c))
+        part_out[y * 4 + q] = gsend[q, pl.ds(pl.multiple_of(y * 64, 64), 64)]
         rn = 1.0 / jnp.sqrt(jnp.sum(s2 + sq[q], axis=1, keepdims=True) + EPS)
         dots = jnp.sum(dd + dt[q], axis=1, keepdims=True)
         qv = qrow[q]
         qn = jnp.sqrt(jnp.sum(jnp.sum(qv * qv, axis=0, keepdims=True), axis=1, keepdims=True) + EPS)
         score = (scale * dots) * (rn / qn)
-        flat = jnp.where(lane == 0, score, rn).T
-        gsend[q] = g * flat[1:2, :]
-        ssend[q] = flat[0:2, :]
-        for d in (1, 3, 2):
-            y2 = up(y, d, NY)
-            remote(gsend.at[q, pl.ds(y2 * 64, 64)], part_out.at[y * 4 + q], gs, gr, dev(y2, z, x, c))
-            remote(ssend.at[q], vec_out.at[y * 4 + q], ss, sr, dev(y2, z, x, c))
-        part_out[y * 4 + q] = gsend[q, pl.ds(pl.multiple_of(y * 64, 64), 64)]
+        ssend[q] = jnp.where(lane == 0, score, rn).T[0:2, :]
+        for d in FAR:
+            remote(ssend.at[q], vec_out.at[y * 4 + q], ss, sr, dev(up(y, d, NY), z, x, c))
         vec_out[y * 4 + q] = ssend[q]
     arrived(part_out.at[0:12], gr)
     arrived(vec_out.at[0:12], sr)
@@ -391,7 +392,7 @@
     part, vec = main_call(math.sqrt(full_width), block_ids, queries, slab.reshape(blocks_each, BLOCK, width_part))
     own = lax.dynamic_slice_in_dim(vec, lax.axis_index("pb") * 64, 64, 2)
     scores = vec[:, 0]
-    gram = part * own[:, 1][:, :, None]
+    gram = part * (own[:, 1][:, :, None] * vec[:, 1][:, None, :])
     penalty = gram * jax.nn.sigmoid(scores[:, None, :] - own[:, 0][:, :, None])
     return (scores, gram, penalty)
 

time: 105 us -> 104 us (level)
  no operation moved by 1% of the time
where the time goes in v5:
time: 104 us
  Pallas kernels  101 us (97%)
  other arithmetic  1.71 us (2%)
    pallas_call x1, Pallas kernels, main_call(): pl.pallas_call(functools.partial(main_kernel, scale), out_shape=(pltpu.VM...  101 us

profile of v5, /device:TPU:1, one launch (start us, length us, event | category | flops | bytes accessed | tf_op | source)
XLA Modules:
  0.0 103.7 jit_solution(6318268012817681435)
XLA Ops:
  0.6 101.1 %shard_map.58 = (f32[16,64,256]{2,1,0:T(8,128)S(1)}, f32[16,2,256]{2,1,0:T(2,128)S(1)}) custom-call(s32[16,16]{1,0:T(8,128)} %ids.1, f32[16,256]{1,0:T(8,128)} %query.1, f32[512,16,256]{2,1,0:T(8,128)} %bitcast.7), custom_call_target="tpu_custom_call" | custom-call | tf_op jit(solution)/shard_map/pallas_call | solution.py:367
  101.8 0.1 constant_dynamic-slice_fusion
  101.9 0.0 copy-start
  102.0 1.7 %divide_multiply_fusion = (f32[16,64,256]{2,1,0:T(8,128)}, f32[16,64,256]{2,1,0:T(8,128)}) fusion(f32[16,64]{1,0:T(8,128)S(1)} %bitcast.9, f32[16,256]{1,0:T(8,128)S(1)} %get-tuple-element.14, f32[16,64,256]{2,1,0:T(8,128)S(1)} %get-tuple-element.6, f32[16,256]{1,0:T(8,128)S(1)} %get-tuple-element.13, f32[16,64]{1,0:T(8,128)S(1)} %bitcast.8), kind=kLoop, calls=%fused_computation | loop fusion | flops 1835008 | bytes 3186688 | tf_op jit(solution)/shard_map/mul | solution.py:396
  103.7 0.0 copy-done
  (2 shorter events, 0.0 us)
Async XLA Ops:
  101.9 1.7 %copy-start = (f32[16,256]{1,0:T(8,128)}, f32[16,256]{1,0:T(8,128)S(1)}, u32[]{:S(2)}) copy-start(f32[16,256]{1,0:T(8,128)S(1)} %get-tuple-element.14) | copy-start | bytes 49156

commit v6 on v5

--- a/solution.py
+++ b/solution.py
@@ -40,14 +40,14 @@
     def up(v, d, n):
         return (v + d) % n
 
+    icopy = pltpu.make_async_copy(ids, idv, isem)
+    icopy.start()
     peers = [dev(y, *at, up(c, e, NC)) for d, e in WIDE if d for at in ((up(z, d, NZ), x), (z, up(x, d, NX)))]
     peers[4:4] = [dev(up(y, d, NY), z, x, c) for d in FAR]
     peers.append(dev(y, z, x, up(c, 1, NC)))
     barrier = pltpu.get_barrier_semaphore()
     for p in peers:
         pl.semaphore_signal(barrier, inc=1, device_id=p, device_id_type=MESH)
-    icopy = pltpu.make_async_copy(ids, idv, isem)
-    icopy.start()
     qcopy = pltpu.make_async_copy(query, qall.at[y], qsem)
     qcopy.start()
     load = pltpu.make_async_copy(slab, slabv, lsem)
@@ -157,12 +157,12 @@
         for d in FAR:
             z2, x2 = up(z, d, NZ), up(x, d, NX)
             mine_a, mine_b = pl.ds(x * NC, NC), pl.ds(z * NC, NC)
-            remote(src_a[0].at[z2, mine_a], mid_a[0].at[z, mine_a], s1s, s1r.at[0, 0], dev(y, z2, x, c))
-            remote(src_b[0].at[x2, mine_b], mid_b[0].at[x, mine_b], s1s, s1r.at[0, 1], dev(y, z, x2, c))
+            remote(src_a[0].at[z2, mine_a], mid_a[0].at[z, mine_a], s1s, s1r.at[0], dev(y, z2, x, c))
+            remote(src_b[0].at[x2, mine_b], mid_b[0].at[x, mine_b], s1s, s1r.at[0], dev(y, z, x2, c))
         for d, e in WIDE:
             z2, x2, c2 = up(z, d, NZ), up(x, d, NX), up(c, e, NC)
-            remote(mid_a[0].at[z, x2 * NC + c2], fin[0].at[z, c, x, 0:HALF], s2s, s2r.at[0, 0], dev(y, z, x2, c2))
-            remote(mid_b[0].at[x, z2 * NC + c2], fin[0].at[z, c, x, HALF:CAP], s2s, s2r.at[0, 1], dev(y, z2, x, c2))
+            remote(mid_a[0].at[z, x2 * NC + c2], fin[0].at[z, c, x, 0:HALF], s2s, s2r.at[0], dev(y, z, x2, c2))
+            remote(mid_b[0].at[x, z2 * NC + c2], fin[0].at[z, c, x, HALF:CAP], s2s, s2r.at[0], dev(y, z2, x, c2))
 
     def open_far():
         for d in range(1, 4):
@@ -180,36 +180,34 @@
             for k2 in range(1, 4):
                 z2, x2 = up(z, d, NZ), up(x, d, NX)
                 their_a, their_b = pl.ds(up(x, k2, NX) * NC, NC), pl.ds(up(z, k2, NZ) * NC, NC)
-                remote(src_a[0].at[z2, their_a], mid_a[0].at[z, their_a], s1s, s1r.at[0, 0], dev(y, z2, x, c))
-                remote(src_b[0].at[x2, their_b], mid_b[0].at[x, their_b], s1s, s1r.at[0, 1], dev(y, z, x2, c))
+                remote(src_a[0].at[z2, their_a], mid_a[0].at[z, their_a], s1s, s1r.at[0], dev(y, z2, x, c))
+                remote(src_b[0].at[x2, their_b], mid_b[0].at[x, their_b], s1s, s1r.at[0], dev(y, z, x2, c))
 
     def stage1(ch):
         gather(ch)
         for d in FAR:
             z2, x2 = up(z, d, NZ), up(x, d, NX)
-            remote(src_a[ch].at[z2], mid_a[ch].at[z], s1s, s1r.at[ch, 0], dev(y, z2, x, c))
-            remote(src_b[ch].at[x2], mid_b[ch].at[x], s1s, s1r.at[ch, 1], dev(y, z, x2, c))
+            remote(src_a[ch].at[z2], mid_a[ch].at[z], s1s, s1r.at[ch], dev(y, z2, x, c))
+            remote(src_b[ch].at[x2], mid_b[ch].at[x], s1s, s1r.at[ch], dev(y, z, x2, c))
 
     def stage2(ch):
-        arrived(mid_a[ch].at[0:3], s1r.at[ch, 0])
-        arrived(mid_b[ch].at[0:3], s1r.at[ch, 1])
+        arrived(slabv.at[0:9 * CHUNKS[ch][0]], s1r.at[ch])
         for d, e in WIDE:
             z2, x2, c2 = up(z, d, NZ), up(x, d, NX), up(c, e, NC)
             if ch:
-                remote(mid_a[ch].at[:, x2 * NC + c2], fin[ch].at[:, c, x, 0:HALF], s2s, s2r.at[ch, 0], dev(y, z, x2, c2))
-                remote(mid_b[ch].at[:, z2 * NC + c2], fin[ch].at[z, c, :, HALF:CAP], s2s, s2r.at[ch, 1], dev(y, z2, x, c2))
+                remote(mid_a[ch].at[:, x2 * NC + c2], fin[ch].at[:, c, x, 0:HALF], s2s, s2r.at[ch], dev(y, z, x2, c2))
+                remote(mid_b[ch].at[:, z2 * NC + c2], fin[ch].at[z, c, :, HALF:CAP], s2s, s2r.at[ch], dev(y, z2, x, c2))
             else:
                 for k2 in range(1, 4):
                     z3, x3 = up(z, k2, NZ), up(x, k2, NX)
-                    remote(mid_a[0].at[z3, x2 * NC + c2], fin[0].at[z3, c, x, 0:HALF], s2s, s2r.at[0, 0], dev(y, z, x2, c2))
-                    remote(mid_b[0].at[x3, z2 * NC + c2], fin[0].at[z, c, x3, HALF:CAP], s2s, s2r.at[0, 1], dev(y, z2, x, c2))
+                    remote(mid_a[0].at[z3, x2 * NC + c2], fin[0].at[z3, c, x, 0:HALF], s2s, s2r.at[0], dev(y, z, x2, c2))
+                    remote(mid_b[0].at[x3, z2 * NC + c2], fin[0].at[z, c, x3, HALF:CAP], s2s, s2r.at[0], dev(y, z2, x, c2))
         for i in range(4):
             fin[ch][i, c, x, 0:HALF] = mid_a[ch][i, jx]
             fin[ch][z, c, i, HALF:CAP] = mid_b[ch][i, jz]
 
     def both_arrived(ch):
-        arrived(mid_a[ch].at[:, 0:7], s2r.at[ch, 0])
-        arrived(mid_b[ch].at[:, 0:7], s2r.at[ch, 1])
+        arrived(slabv.at[0:21 * CHUNKS[ch][0] // 2], s2r.at[ch])
 
     def pick(ch, y2, q, out):
         flat = fin[ch].reshape(NZ * NC * NX * CAP, CHUNKS[ch][0], 128)
@@ -379,7 +377,7 @@
             *[vm((NY, 64, n, 128), F32) for n in sizes],
             vm((4, 256, 256), F32), vm((4, 256, 128), F32), vm((4, 256, 128), F32),
             vm((4, 256, 256), F32), vm((4, 2, 256), F32),
-            *[dma(()) for _ in range(13)], dma((NCH, 2)), dma(()), dma((NCH, 2)), dma(()), dma((NCH,)), dma((4,)), *[dma(()) for _ in range(4)],
+            *[dma(()) for _ in range(13)], dma((NCH,)), dma(()), dma((NCH,)), dma(()), dma((NCH,)), dma((4,)), *[dma(()) for _ in range(4)],
         ],
         compiler_params=pltpu.CompilerParams(collective_id=0, has_side_effects=True, vmem_limit_bytes=58 * 2**20),
     )(ids, query, slab)

time: 104 us -> 104 us (level)
  no operation moved by 1% of the time
where the time goes in v6:
time: 104 us
  Pallas kernels  101 us (97%)
  other arithmetic  1.71 us (2%)
    pallas_call x1, Pallas kernels, main_call(): pl.pallas_call(functools.partial(main_kernel, scale), out_shape=(pltpu.VM...  101 us

profile of v6, /device:TPU:1, one launch (start us, length us, event | category | flops | bytes accessed | tf_op | source)
XLA Modules:
  0.0 103.5 jit_solution(8277205757291775851)
XLA Ops:
  0.6 101.0 %shard_map.58 = (f32[16,64,256]{2,1,0:T(8,128)S(1)}, f32[16,2,256]{2,1,0:T(2,128)S(1)}) custom-call(s32[16,16]{1,0:T(8,128)} %ids.1, f32[16,256]{1,0:T(8,128)} %query.1, f32[512,16,256]{2,1,0:T(8,128)} %bitcast.7), custom_call_target="tpu_custom_call" | custom-call | tf_op jit(solution)/shard_map/pallas_call | solution.py:365
  101.6 0.1 constant_dynamic-slice_fusion
  101.8 0.0 copy-start
  101.8 1.7 %divide_multiply_fusion = (f32[16,64,256]{2,1,0:T(8,128)}, f32[16,64,256]{2,1,0:T(8,128)}) fusion(f32[16,64]{1,0:T(8,128)S(1)} %bitcast.9, f32[16,256]{1,0:T(8,128)S(1)} %get-tuple-element.14, f32[16,64,256]{2,1,0:T(8,128)S(1)} %get-tuple-element.6, f32[16,256]{1,0:T(8,128)S(1)} %get-tuple-element.13, f32[16,64]{1,0:T(8,128)S(1)} %bitcast.8), kind=kLoop, calls=%fused_computation | loop fusion | flops 1835008 | bytes 3186688 | tf_op jit(solution)/shard_map/mul | solution.py:394
  103.5 0.0 copy-done
  (2 shorter events, 0.0 us)
Async XLA Ops:
  101.8 1.7 %copy-start = (f32[16,256]{1,0:T(8,128)}, f32[16,256]{1,0:T(8,128)S(1)}, u32[]{:S(2)}) copy-start(f32[16,256]{1,0:T(8,128)S(1)} %get-tuple-element.14) | copy-start | bytes 49156

commit v7 on v6

--- a/solution.py
+++ b/solution.py
@@ -140,6 +140,12 @@
 
             lax.fori_loop(0, 8, body, 0)
 
+    def own_pieces(ch):
+        for d, e in WIDE:
+            z2, x2, c2 = up(z, d, NZ), up(x, d, NX), up(c, e, NC)
+            remote(mid_a[ch].at[z, x2 * NC + c2], fin[ch].at[z, c, x, 0:HALF], s2s, s2r.at[ch], dev(y, z, x2, c2))
+            remote(mid_b[ch].at[x, z2 * NC + c2], fin[ch].at[z, c, x, HALF:CAP], s2s, s2r.at[ch], dev(y, z2, x, c2))
+
     def open_near():
         for d in range(4):
             z2, x2 = up(z, d, NZ), up(x, d, NX)
@@ -159,10 +165,7 @@
             mine_a, mine_b = pl.ds(x * NC, NC), pl.ds(z * NC, NC)
             remote(src_a[0].at[z2, mine_a], mid_a[0].at[z, mine_a], s1s, s1r.at[0], dev(y, z2, x, c))
             remote(src_b[0].at[x2, mine_b], mid_b[0].at[x, mine_b], s1s, s1r.at[0], dev(y, z, x2, c))
-        for d, e in WIDE:
-            z2, x2, c2 = up(z, d, NZ), up(x, d, NX), up(c, e, NC)
-            remote(mid_a[0].at[z, x2 * NC + c2], fin[0].at[z, c, x, 0:HALF], s2s, s2r.at[0], dev(y, z, x2, c2))
-            remote(mid_b[0].at[x, z2 * NC + c2], fin[0].at[z, c, x, HALF:CAP], s2s, s2r.at[0], dev(y, z2, x, c2))
+        own_pieces(0)
 
     def open_far():
         for d in range(1, 4):
@@ -189,19 +192,21 @@
             z2, x2 = up(z, d, NZ), up(x, d, NX)
             remote(src_a[ch].at[z2], mid_a[ch].at[z], s1s, s1r.at[ch], dev(y, z2, x, c))
             remote(src_b[ch].at[x2], mid_b[ch].at[x], s1s, s1r.at[ch], dev(y, z, x2, c))
+        if ch == NCH - 1:
+            own_pieces(ch)
 
     def stage2(ch):
         arrived(slabv.at[0:9 * CHUNKS[ch][0]], s1r.at[ch])
         for d, e in WIDE:
             z2, x2, c2 = up(z, d, NZ), up(x, d, NX), up(c, e, NC)
-            if ch:
+            if ch not in (0, NCH - 1):
                 remote(mid_a[ch].at[:, x2 * NC + c2], fin[ch].at[:, c, x, 0:HALF], s2s, s2r.at[ch], dev(y, z, x2, c2))
                 remote(mid_b[ch].at[:, z2 * NC + c2], fin[ch].at[z, c, :, HALF:CAP], s2s, s2r.at[ch], dev(y, z2, x, c2))
             else:
                 for k2 in range(1, 4):
                     z3, x3 = up(z, k2, NZ), up(x, k2, NX)
-                    remote(mid_a[0].at[z3, x2 * NC + c2], fin[0].at[z3, c, x, 0:HALF], s2s, s2r.at[0], dev(y, z, x2, c2))
-                    remote(mid_b[0].at[x3, z2 * NC + c2], fin[0].at[z, c, x3, HALF:CAP], s2s, s2r.at[0], dev(y, z2, x, c2))
+                    remote(mid_a[ch].at[z3, x2 * NC + c2], fin[ch].at[z3, c, x, 0:HALF], s2s, s2r.at[ch], dev(y, z, x2, c2))
+                    remote(mid_b[ch].at[x3, z2 * NC + c2], fin[ch].at[z, c, x3, HALF:CAP], s2s, s2r.at[ch], dev(y, z2, x, c2))
         for i in range(4):
             fin[ch][i, c, x, 0:HALF] = mid_a[ch][i, jx]
             fin[ch][z, c, i, HALF:CAP] = mid_b[ch][i, jz]

time: 104 us -> 104 us (level)
  no operation moved by 1% of the time
where the time goes in v7:
time: 104 us
  Pallas kernels  101 us (97%)
  other arithmetic  1.71 us (2%)
    pallas_call x1, Pallas kernels, main_call(): pl.pallas_call(functools.partial(main_kernel, scale), out_shape=(pltpu.VM...  101 us

profile of v7, /device:TPU:1, one launch (start us, length us, event | category | flops | bytes accessed | tf_op | source)
XLA Modules:
  0.0 103.6 jit_solution(3036598364408964551)
XLA Ops:
  0.6 101.0 %shard_map.58 = (f32[16,64,256]{2,1,0:T(8,128)S(1)}, f32[16,2,256]{2,1,0:T(2,128)S(1)}) custom-call(s32[16,16]{1,0:T(8,128)} %ids.1, f32[16,256]{1,0:T(8,128)} %query.1, f32[512,16,256]{2,1,0:T(8,128)} %bitcast.7), custom_call_target="tpu_custom_call" | custom-call | tf_op jit(solution)/shard_map/pallas_call | solution.py:370
  101.7 0.1 constant_dynamic-slice_fusion
  101.8 0.0 copy-start
  101.9 1.7 %divide_multiply_fusion = (f32[16,64,256]{2,1,0:T(8,128)}, f32[16,64,256]{2,1,0:T(8,128)}) fusion(f32[16,64]{1,0:T(8,128)S(1)} %bitcast.9, f32[16,256]{1,0:T(8,128)S(1)} %get-tuple-element.14, f32[16,64,256]{2,1,0:T(8,128)S(1)} %get-tuple-element.6, f32[16,256]{1,0:T(8,128)S(1)} %get-tuple-element.13, f32[16,64]{1,0:T(8,128)S(1)} %bitcast.8), kind=kLoop, calls=%fused_computation | loop fusion | flops 1835008 | bytes 3186688 | tf_op jit(solution)/shard_map/mul | solution.py:399
  103.6 0.0 copy-done
  (2 shorter events, 0.0 us)
Async XLA Ops:
  101.8 1.7 %copy-start = (f32[16,256]{1,0:T(8,128)}, f32[16,256]{1,0:T(8,128)S(1)}, u32[]{:S(2)}) copy-start(f32[16,256]{1,0:T(8,128)S(1)} %get-tuple-element.14) | copy-start | bytes 49156
